TPU v7x, 32 devices: a whole 2x2x4 slice. The times are simulated.
32 devices in a mesh: col: 4 (over z), row: 8 (over y, x, core).
Axes of the slice: x: 2, y: 2, z: 4, core: 2. Of those that a mesh axis runs over, the one named last changes fastest.
Arguments:
- vel_u: float32 [62, 1024, 256], P(None, 'row', 'col')
- vel_v: float32 [62, 1024, 256], P(None, 'row', 'col')
- temperature: float32 [62, 1024, 256], P(None, 'row', 'col')
- salinity: float32 [62, 1024, 256], P(None, 'row', 'col')
- sea_level: float32 [1024, 256], P('row', 'col')
- trans_u: float32 [1024, 256], P('row', 'col')
- trans_v: float32 [1024, 256], P('row', 'col')
- col_depth: float32 [1024, 256], P('row', 'col')
- kmt_levels: int32 [1024, 256], P('row', 'col')
Outputs:
- output 1: float32 [1024, 256], P('row', 'col')
- output 2: float32 [1024, 256], P('row', 'col')
- output 3: float32 [1024, 256], P('row', 'col')
- output 4: float32 [62, 1024, 256], P(None, 'row', 'col')
- output 5: float32 [62, 1024, 256], P(None, 'row', 'col')
- output 6: float32 [62, 1024, 256], P(None, 'row', 'col')
- output 7: float32 [62, 1024, 256], P(None, 'row', 'col')
All inputs are finite; a program needn't handle non-finite values.
Results may differ from a plain program's by a relative error of at most 0.001.
Values sent between devices are 32-bit elements.
A program may use at most 1 GiB of HBM per device.

v0:
```python
import functools
import itertools

import jax
import jax.numpy as jnp
import numpy as np
from jax import lax
from jax.experimental import pallas as pl
from jax.experimental.pallas import tpu as pltpu
from jax.sharding import PartitionSpec as P

LEVELS = 62
NI = 64
NJ = 128
HALO = 32
SUBCYCLES = 30
ADV_COURANT = 0.25
WAVE_COURANT = 0.5
VISC_NUM = 4.0
DIFF_NUM = 1.0
ALPHA_T = 0.3
BETA_S = 0.6

F32 = jnp.float32
MESH = pl.DeviceIdType.MESH
VMEM = pltpu.VMEM
OFF = 8
IPAD = NI + 16
IEXT = NI + 2 * HALO
JEXT = NJ + 2 * HALO
EAST, WEST = slice(NI - 1, NI), slice(0, 1)
OWN = slice(OFF, OFF + NI)
WEST_HALO, EAST_HALO = slice(OFF - 1, OFF), slice(OFF + NI, OFF + NI + 1)
BEFORE, AFTER = slice(0, OFF), slice(OFF + NI, IPAD)
CORE = slice(HALO, HALO + NI)
LOW, HIGH = slice(0, HALO), slice(HALO + NI, IEXT)
FAR_EAST, FAR_WEST = slice(NI - HALO, NI), slice(0, HALO)


def solve_constants(diff):
    ratio, inner, last = [], [], []
    c_prev = 0.0
    for k in range(LEVELS):
        lower = diff if k > 0 else 0.0
        pivot = 1.0 + diff + lower - lower * c_prev
        inner.append(1.0 / pivot)
        last.append(1.0 / (1.0 + lower - lower * c_prev))
        c_prev = diff / pivot
        ratio.append(c_prev)
    return ratio, inner, last


RATIO_V, INNER_V, LAST_V = solve_constants(VISC_NUM)
RATIO_D, INNER_D, LAST_D = solve_constants(DIFF_NUM)


def sm_weights():
    s = np.arange(1, SUBCYCLES + 1, dtype=np.float64) / (SUBCYCLES + 1)
    raw = s ** 2 * (1.0 - s ** 4)
    return raw / np.sum(raw)


WEIGHTS = sm_weights()
TAIL_WEIGHTS = np.cumsum(WEIGHTS[::-1])[::-1]
MEAN_STEP = float(np.sum(WEIGHTS * np.arange(1, SUBCYCLES + 1)))
MESSAGES = 38
LAG = 7
CHUNK = 24


def rot(x, shift):
    shift = shift % x.shape[-1]
    return pltpu.roll(x, shift, 1) if shift else x


def back(x):
    return rot(x, 1)


def ahead(x):
    return rot(x, -1)


def keep(mask, x):
    return jnp.where(mask, x, 0.0)


def pos(x):
    return jnp.maximum(x, 0.0)


def neg(x):
    return jnp.minimum(x, 0.0)


def per_level(x, count):
    return x / jnp.maximum(count, 1.0)


ETA, TU, TV, DEP, KMT = range(5)
U, V, T, S, MEAN, PRES, T_FLUX, S_FLUX = range(8)
UV, TS = range(2)


def exchange_kernel(
    col_count, row_count,
    u_hbm, v_hbm, t_hbm, s_hbm, eta_hbm, tu_hbm, tv_hbm, dep_hbm, kmt_hbm,
    du_o, dv_o, dt_o, ds_o, flat_o,
    u3, v3, t3, s3, p3, un3, us3, vn3, vs3, tn3, sn3, st2, near_w, near_e, kmt_i, ext2, pk2n, pk2s, hs2, hn2,
    pack, mn, ms, in_s, in_n, rr,
    ff, extf, pkfn, pkfs, hsf, hnf,
    kmu, kmw, kmv, hu2, hv2, smr,
    b_e0, b_e1, b_d, b_p, b_wu, b_ww, b_wv, b_u, b_v, b_pu, b_pv, b_s, b_g,
    ld3, ld2, snd, rcv,
):
    c = lax.axis_index("col")
    r = lax.axis_index("row")
    has_n = r < row_count - 1
    has_s = r > 0
    label = itertools.count()
    east = lax.rem(c + 1, col_count)
    west = lax.rem(c + col_count - 1, col_count)
    up, down = r + 1, r - 1

    barrier = pltpu.get_barrier_semaphore()

    def greet(cc, row):
        pl.semaphore_signal(barrier, inc=1, device_id=(cc, row), device_id_type=MESH)

    greet(east, r)
    greet(west, r)

    @pl.when(has_n)
    def _():
        for cc in (west, c, east):
            greet(cc, up)

    @pl.when(has_s)
    def _():
        for cc in (west, c, east):
            greet(cc, down)

    loads2 = []
    for f, src in enumerate((eta_hbm, tu_hbm, tv_hbm, dep_hbm)):
        loads2.append(pltpu.make_async_copy(src, st2.at[f, :NI, :], ld2.at[f]))
    loads2.append(pltpu.make_async_copy(kmt_hbm, kmt_i, ld2.at[KMT]))
    loads3 = []
    for f, (src, dst) in enumerate(((t_hbm, t3), (s_hbm, s3), (u_hbm, u3), (v_hbm, v3))):
        loads3.append(pltpu.make_async_copy(src, dst.at[:, OWN, :], ld3.at[f]))
    for cp in loads2 + loads3[:2]:
        cp.start()

    def remote(src, dst, cc, row):
        n = next(label)
        return pltpu.make_async_remote_copy(
            src_ref=src, dst_ref=dst, send_sem=snd.at[n], recv_sem=rcv.at[n],
            device_id=(cc, row), device_id_type=MESH)

    def each(go_ew, ew, cond_n, go_n, no, cond_s, so):
        for cp in ew:
            go_ew(cp)
        if no:
            @pl.when(cond_n)
            def _():
                for cp in no:
                    go_n(cp)
        if so:
            @pl.when(cond_s)
            def _():
                for cp in so:
                    go_n(cp)

    def start(ew=(), no=(), so=()):
        go = lambda cp: cp.start()
        each(go, ew, has_n, go, no, has_s, so)

    def recv(ew=(), no=(), so=()):
        go = lambda cp: cp.wait_recv()
        each(go, ew, has_s, go, no, has_n, so)

    def sent(ew=(), no=(), so=()):
        go = lambda cp: cp.wait_send()
        each(go, ew, has_n, go, no, has_s, so)

    g1 = []
    for src, dst in ((u_hbm, u3), (v_hbm, v3), (t_hbm, t3), (s_hbm, s3)):
        g1.append(remote(src.at[:, EAST, :], dst.at[:, WEST_HALO, :], east, r))
        g1.append(remote(src.at[:, WEST, :], dst.at[:, EAST_HALO, :], west, r))

    def near_ns(pn, ps, hs, hn):
        if hs.shape[0] > NI:
            hs, hn = hs.at[CORE, :], hn.at[CORE, :]
        return [remote(pn, hs, c, up)], [remote(ps, hn, c, down)]

    def corners(pn, ps, hs, hn):
        no = [
            remote(pn.at[FAR_EAST, :], hs.at[LOW, :], east, up),
            remote(pn.at[FAR_WEST, :], hs.at[HIGH, :], west, up),
        ]
        so = [
            remote(ps.at[FAR_EAST, :], hn.at[LOW, :], east, down),
            remote(ps.at[FAR_WEST, :], hn.at[HIGH, :], west, down),
        ]
        return no, so

    def side_ew(own, ext):
        return [
            remote(own.at[:, FAR_EAST, :], ext.at[:, LOW, :], east, r),
            remote(own.at[:, FAR_WEST, :], ext.at[:, HIGH, :], west, r),
        ]

    lane64 = lax.broadcasted_iota(jnp.int32, (NI, NJ), 1)
    group64 = lane64 // HALO

    def pack_flat(fields, src, pn, ps):
        top = jnp.zeros((NI, NJ), F32)
        bot = jnp.zeros((NI, NJ), F32)
        for q, f in enumerate(fields):
            x = src[f, :NI, :]
            top = jnp.where(group64 == q, rot(x, HALO * q + HALO), top)
            bot = jnp.where(group64 == q, rot(x, HALO * q), bot)
        pn[...] = top
        ps[...] = bot

    for cp in loads2:
        cp.wait()
    for cp in loads3[2:]:
        cp.start()
    st2[KMT, :NI, :] = kmt_i[...].astype(F32)
    for f in (DEP, KMT):
        st2[f, NI:, :] = jnp.zeros((OFF, NJ), F32)
    near2 = pk2n.at[1], pk2s.at[1], hs2.at[1], hn2.at[1]
    far2 = pk2n.at[0], pk2s.at[0], hs2.at[0], hn2.at[0]
    pack_flat((DEP, KMT), st2, *near2[:2])
    pack_flat((ETA, TU, TV), st2, *far2[:2])
    for f in range(5):
        ext2[f, CORE, :] = st2[f, :NI, :]

    lane8 = lax.broadcasted_iota(jnp.int32, (8, NJ), 1)
    first8 = lane8 == 0
    last8 = lane8 == NJ - 1
    slot64 = lane64 >> 1
    even64 = (lane64 & 1) == 0

    def rows(ib, off=0):
        return pl.ds(pl.multiple_of(ib * 8, 8) + off, 8)

    def pack_edges(f, ref):
        acc = jnp.zeros((NI, NJ), F32)
        for k in range(LEVELS):
            acc = jnp.where(slot64 == k, rot(ref[k, OWN, :], 2 * k + 1), acc)
        pack[f] = acc

    def pack_pair(a):
        x, y = pack[2 * a], pack[2 * a + 1]
        mn[a] = jnp.where(even64, y, back(x))
        ms[a] = jnp.where(even64, ahead(x), y)

    loads3[0].wait()
    pack_edges(T, t3)

    pl.semaphore_wait(barrier, 2 + 3 * has_n.astype(jnp.int32) + 3 * has_s.astype(jnp.int32))
    g0 = [
        remote(st2.at[DEP:KMT + 1, EAST, :], near_w.at[:, WEST, :], east, r),
        remote(st2.at[DEP:KMT + 1, WEST, :], near_e.at[:, WEST, :], west, r),
    ]
    g2b_n, g2b_s = near_ns(*near2)
    start(g0 + g1, g2b_n, g2b_s)

    loads3[1].wait()
    pack_edges(S, s3)
    pack_pair(TS)
    g3n, g3s = near_ns(mn.at[TS], ms.at[TS], in_s.at[TS, OWN, :], in_n.at[TS, OWN, :])
    start((), g3n, g3s)
    loads3[2].wait()
    pack_edges(U, u3)
    loads3[3].wait()
    pack_edges(V, v3)
    pack_pair(UV)
    g5n, g5s = near_ns(mn.at[UV], ms.at[UV], in_s.at[UV, OWN, :], in_n.at[UV, OWN, :])
    g7n = [remote(mn.at[UV, :OFF, :], in_s.at[UV, AFTER, :], west, up)]
    g7s = [remote(ms.at[UV, NI - OFF:NI, :], in_n.at[UV, BEFORE, :], east, down)]
    start((), g5n + g7n, g5s + g7s)
    g2 = side_ew(st2, ext2)
    g2a_n, g2a_s = near_ns(*far2)
    gc_n, gc_s = corners(*near2)
    gd_n, gd_s = corners(*far2)
    start(g2, g2a_n + gc_n + gd_n, g2a_s + gc_s + gd_s)

    def local_body(ib, carry):
        mid, at = rows(ib, OFF), rows(ib)
        km = st2[KMT, at, :]
        thick = per_level(st2[DEP, at, :], km)
        total = jnp.zeros((8, NJ), F32)
        for k in range(LEVELS):
            u, v = u3[k, mid, :], v3[k, mid, :]
            un3[k, mid, :] = ahead(u)
            us3[k, at, :] = back(u)
            vn3[k, at, :] = ahead(v)
            vs3[k, mid, :] = back(v)
            dens = keep(km > k, BETA_S * s3[k, mid, :] - ALPHA_T * t3[k, mid, :])
            total = total + dens
            p3[k, mid, :] = (total - 0.5 * dens) * thick
        return carry
    blocks = NI // 8
    lax.fori_loop(0, blocks, local_body, 0)

    recv((), g2b_n, g2b_s)
    has_nf = keep(has_n, 1.0).astype(F32)
    has_sf = keep(has_s, 1.0).astype(F32)
    big_n = jnp.full((NI, 1), has_nf) > 0.5
    big_s = jnp.full((NI, 1), has_sf) > 0.5
    kmt = st2[KMT, :NI, :]
    depth = st2[DEP, :NI, :]
    dep_n = keep(big_n, hn2[1, CORE, 0:1])
    kmt_n = keep(big_n, hn2[1, CORE, HALO:HALO + 1])
    kmt_s = keep(big_s, hs2[1, CORE, 2 * HALO - 1:2 * HALO])
    last64 = lane64 == NJ - 1
    kmt_north = jnp.where(last64, kmt_n, ahead(kmt))
    dep_north = jnp.where(last64, dep_n, ahead(depth))
    kmv_v = jnp.minimum(kmt, kmt_north)
    kmv[...] = kmv_v
    hv2[...] = keep(kmv_v > 0, 0.5 * (depth + dep_north))

    def u_faces():
        kmu_v = jnp.minimum(st2[KMT, :NI, :], st2[KMT, 1:NI + 1, :])
        kmu[...] = kmu_v
        hu2[...] = keep(kmu_v > 0, 0.5 * (st2[DEP, :NI, :] + st2[DEP, 1:NI + 1, :]))

    u_faces()

    def unpack_pair(a, where):
        north = keep(has_nf > 0.5, in_n[a, where, :])
        south = keep(has_sf > 0.5, in_s[a, where, :])
        even = (lax.broadcasted_iota(jnp.int32, north.shape, 1) & 1) == 0
        rr[2 * a, where, :] = jnp.where(even, north, south)
        rr[2 * a + 1, where, :] = jnp.where(even, ahead(north), back(south))

    def mean_rows():
        mean_n = rr[U, OWN, :] + rr[U, OFF - 1:OFF + NI - 1, :]
        mean_s = rr[V, OWN, :] + rr[V, OFF + 1:OFF + NI + 1, :]
        rr[MEAN, OWN, :] = jnp.where(even64, mean_n, mean_s)

    recv((), g3n, g3s)
    unpack_pair(TS, OWN)
    rt, rs = rr[T, OWN, :], rr[S, OWN, :]
    dens = keep((kmt_n > slot64.astype(F32)) & even64, BETA_S * rs - ALPHA_T * rt)
    above = lax.broadcasted_iota(jnp.int32, (NJ, NJ), 0) <= lax.broadcasted_iota(jnp.int32, (NJ, NJ), 1)
    total = jnp.dot(dens, above.astype(F32), precision=lax.Precision.HIGHEST, preferred_element_type=F32)
    rr[PRES, OWN, :] = (total - 0.5 * dens) * per_level(dep_n, kmt_n)
    recv((), g5n, g5s)
    rr[U, BEFORE, :] = jnp.zeros((OFF, NJ), F32)
    rr[V, AFTER, :] = jnp.zeros((OFF, NJ), F32)
    unpack_pair(UV, OWN)
    mean_rows()
    rv = rr[V, OWN, :]
    face_s = jnp.minimum(kmt_s, kmt[:, 0:1]) > slot64.astype(F32)
    vs_pos = keep(face_s, pos(rv))
    vs_neg = keep(face_s, neg(rv))
    rr[T_FLUX, OWN, :] = jnp.where(even64, rt, vs_pos * rt + vs_neg * pack[T])
    rr[S_FLUX, OWN, :] = jnp.where(even64, rs, vs_pos * rs + vs_neg * pack[S])

    def momentum_body(ib):
        at, mid, below, above = rows(ib), rows(ib, OFF), rows(ib, OFF - 1), rows(ib, OFF + 1)
        km_u = kmu[at, :]
        km_v = kmv[at, :]
        qu, qv, qm, qp = (rr[f, mid, :] for f in (U, V, MEAN, PRES))
        zero = jnp.zeros((8, NJ), F32)
        du, dv, st_u, st_v, sr_u, sr_v = (zero,) * 6
        for k in range(LEVELS):
            sh = NJ - 1 - 2 * k
            hu, hv, hm, hp = rot(qu, sh), rot(qv, sh), rot(qm, sh), rot(qp, sh)
            u = u3[k, mid, :]
            ue = u3[k, above, :]
            uw = u3[k, below, :]
            v = v3[k, mid, :]
            ve = v3[k, above, :]
            vw = v3[k, below, :]
            p = p3[k, mid, :]
            pe = p3[k, above, :]
            un_k, vs_k = un3[k, mid, :], vs3[k, mid, :]
            un = jnp.where(last8, hu, un_k)
            us = jnp.where(first8, hu, us3[k, at, :])
            vn = jnp.where(last8, hv, vn3[k, at, :])
            vs = jnp.where(first8, hv, vs_k)
            vm4 = (v + ve) + jnp.where(first8, hm, vs_k + vs3[k, above, :])
            um4 = (u + uw) + jnp.where(last8, hm, un_k + un3[k, below, :])
            pn = jnp.where(last8, hp, ahead(p))
            tn3[k, at, :] = ahead(t3[k, mid, :])
            sn3[k, at, :] = ahead(s3[k, mid, :])
            tu = (p - pe) - 0.5 * (u * (ue - uw)) - 0.125 * (vm4 * (un - us))
            tv = (p - pn) - 0.125 * (um4 * (ve - vw)) - 0.5 * (v * (vn - vs))
            wu = km_u > k
            wv = km_v > k
            tu = keep(wu, tu)
            tv = keep(wv, tv)
            ru_k = keep(wu, u) + ADV_COURANT * tu
            rv_k = keep(wv, v) + ADV_COURANT * tv
            st_u = st_u + tu
            st_v = st_v + tv
            sr_u = sr_u + ru_k
            sr_v = sr_v + rv_k
            fu = jnp.where(km_u > k + 1, INNER_V[k], keep(wu, LAST_V[k]))
            fv = jnp.where(km_v > k + 1, INNER_V[k], keep(wv, LAST_V[k]))
            if k > 0:
                ru_k = ru_k + VISC_NUM * du
                rv_k = rv_k + VISC_NUM * dv
            du = ru_k * fu
            dv = rv_k * fv
            du_o[k, at, :] = du
            dv_o[k, at, :] = dv
        inv_u = per_level(1.0, km_u)
        inv_v = per_level(1.0, km_v)
        ff[0, at, :] = hu2[at, :] * inv_u * st_u
        ff[1, at, :] = hv2[at, :] * inv_v * st_v
        smr[0, at, :] = inv_u * sr_u
        smr[1, at, :] = inv_v * sr_v

    def beside():
        recv(g0 + g1, g7n, g7s)
        for n, f in enumerate((DEP, KMT)):
            st2[f, NI:NI + 1, :] = near_e[n, WEST, :]
        u_faces()
        kmt = st2[KMT, :NI, :]
        first_col = lax.broadcasted_iota(jnp.int32, (NI, NJ), 0) == 0
        kmw[...] = jnp.minimum(kmt, jnp.where(first_col, near_w[1, WEST, :], pltpu.roll(kmt, 1, 0)))
        unpack_pair(UV, BEFORE)
        unpack_pair(UV, AFTER)
        mean_rows()
        km_e = near_e[1, WEST, :]
        thick_e = per_level(near_e[0, WEST, :], km_e)
        tot_e = jnp.zeros((1, NJ), F32)
        for k in range(LEVELS):
            un3[k, WEST_HALO, :] = ahead(u3[k, WEST_HALO, :])
            vs3[k, EAST_HALO, :] = back(v3[k, EAST_HALO, :])
            dens_e = keep(km_e > k, BETA_S * s3[k, EAST_HALO, :] - ALPHA_T * t3[k, EAST_HALO, :])
            tot_e = tot_e + dens_e
            p3[k, EAST_HALO, :] = (tot_e - 0.5 * dens_e) * thick_e

    def loop_body(n, carry):
        pl.when(n == blocks - 2)(beside)
        momentum_body(lax.rem(n + 1, blocks))
        return carry
    lax.fori_loop(0, blocks, loop_body, 0)

    force = pkfn.at[0], pkfs.at[0], hsf.at[0], hnf.at[0]
    pack_flat((0, 1), ff, *force[:2])
    g4 = side_ew(ff, extf)
    g4_n, g4_s = near_ns(*force)
    g6_n, g6_s = corners(*force)
    start(g4, g6_n + g4_n, g6_s + g4_s)
    for f in range(2):
        extf[f, CORE, :] = ff[f]

    def tracer_body(ib, carry):
        at, mid, below, above = rows(ib), rows(ib, OFF), rows(ib, OFF - 1), rows(ib, OFF + 1)
        km_u = kmu[at, :]
        km_w = kmw[at, :]
        km_v = kmv[at, :]
        km = st2[KMT, at, :]
        fields = ((t3, tn3, rr[T_FLUX, mid, :], dt_o), (s3, sn3, rr[S_FLUX, mid, :], ds_o))
        prev = [None, None]
        turned, flux = {}, {}
        for step in range(LEVELS + 2 * LAG):
            k = step
            if k < LEVELS:
                sh = NJ - 1 - 2 * k
                turned[k] = [(rot(q, sh), rot(q, sh - 1)) for _, _, q, _ in fields]
            k = step - LAG
            if 0 <= k < LEVELS:
                v = keep(km_v > k, v3[k, mid, :])
                v_pos, v_neg = pos(v), neg(v)
                flux[k] = []
                for (ref, next_ref, _, _), (north, south) in zip(fields, turned.pop(k)):
                    xn = jnp.where(last8, north, next_ref[k, at, :])
                    fn = v_pos * ref[k, mid, :] + v_neg * xn
                    flux[k].append((fn, back(jnp.where(last8, south, fn))))
            k = step - 2 * LAG
            if k >= 0:
                u = keep(km_u > k, u3[k, mid, :])
                w = keep(km_w > k, u3[k, below, :])
                u_pos, u_neg = pos(u), neg(u)
                w_pos, w_neg = pos(w), neg(w)
                fac = jnp.where(km > k + 1, INNER_D[k], keep(km > k, LAST_D[k]))
                for n, ((ref, _, _, out), (fn, fs)) in enumerate(zip(fields, flux.pop(k))):
                    x = ref[k, mid, :]
                    fe = u_pos * x + u_neg * ref[k, above, :]
                    fw = w_pos * ref[k, below, :] + w_neg * x
                    rhs = x - ADV_COURANT * ((fe - fw) + (fn - fs))
                    if k > 0:
                        rhs = rhs + DIFF_NUM * prev[n]
                    prev[n] = rhs * fac
                    out[k, at, :] = prev[n]
        return carry
    lax.fori_loop(0, blocks, tracer_body, 0)

    recv(g2, g2a_n + gc_n + gd_n, g2a_s + gc_s + gd_s)
    low_ok = jnp.full((HALO, IEXT), has_sf) > 0.5
    high_ok = jnp.full((HALO, IEXT), has_nf) > 0.5

    def window(ext, hs, hn, q):
        low = keep(low_ok, hs[HALO * q:HALO * (q + 1)])
        high = keep(high_ok, hn[HALO * q:HALO * (q + 1)])
        return jnp.concatenate([low, ext.T, high], axis=0)

    hs_t = [hs2[a].T for a in range(2)]
    hn_t = [hn2[a].T for a in range(2)]
    win = pl.ds(8, JEXT)
    north_of = pl.ds(9, JEXT)
    south_of = pl.ds(7, JEXT)
    zpad = jnp.zeros((8, IEXT), F32)
    for ref in (b_e0, b_e1, b_wv, b_v, b_pv, b_s, b_g):
        ref[0:8, :] = zpad
        ref[8 + JEXT:16 + JEXT, :] = zpad
    b_s[win, :] = window(ext2[KMT], hs_t[1], hn_t[1], 1)
    b_g[win, :] = window(ext2[DEP], hs_t[1], hn_t[1], 0)
    km_w = b_s[win, :]
    dp_w = b_g[win, :]
    wet_u = jnp.minimum(km_w, ahead(km_w)) > 0
    wet_v = jnp.minimum(km_w, b_s[north_of, :]) > 0
    wu = keep(wet_u, (0.25 * WAVE_COURANT) * (dp_w + ahead(dp_w)))
    wv = keep(wet_v, (0.25 * WAVE_COURANT) * (dp_w + b_g[north_of, :]))
    b_wu[...] = wu
    b_ww[...] = back(wu)
    b_wv[win, :] = wv
    b_e0[win, :] = keep(km_w > 0, window(ext2[ETA], hs_t[0], hn_t[0], ETA))
    u0 = keep(wet_u, window(ext2[TU], hs_t[0], hn_t[0], TU))
    v0 = keep(wet_v, window(ext2[TV], hs_t[0], hn_t[0], TV))
    b_u[...] = u0
    b_v[win, :] = v0
    b_d[...] = -WAVE_COURANT * ((u0 - back(u0)) + (v0 - b_v[south_of, :]))

    recv(g4, g4_n + g6_n, g4_s + g6_s)
    hsf_t = hsf[0].T
    hnf_t = hnf[0].T
    push = ADV_COURANT / SUBCYCLES
    pu = keep(wet_u, push * window(extf[0], hsf_t, hnf_t, 0))
    pv = keep(wet_v, push * window(extf[1], hsf_t, hnf_t, 1))
    b_pu[...] = pu
    b_pv[win, :] = pv
    b_p[...] = -WAVE_COURANT * ((pu - back(pu)) + (pv - b_pv[south_of, :]))

    eta_bufs = (b_e0, b_e1)
    turned = {}
    for n in range(1, SUBCYCLES + 1):
        old, new = eta_bufs[(n - 1) % 2], eta_bufs[n % 2]
        fresh = {}
        for ch in range(JEXT // CHUNK):
            lo = CHUNK * ch
            if lo + CHUNK - 1 < HALO - (SUBCYCLES - n) or lo > HALO + NJ + (SUBCYCLES - n):
                continue
            here = pl.ds(lo, CHUNK)
            mid = pl.ds(8 + lo, CHUNK)
            e = old[mid, :]
            d = b_d[here, :]
            if n > 1:
                ee, ew = turned[ch]
                gain = b_wu[here, :] * (ee - e) - b_ww[here, :] * (e - ew)
                gain = gain + b_wv[mid, :] * (old[pl.ds(9 + lo, CHUNK), :] - e)
                gain = gain - b_wv[pl.ds(7 + lo, CHUNK), :] * (e - old[pl.ds(7 + lo, CHUNK), :])
                d = d + (gain + b_p[here, :])
                b_d[here, :] = d
            e = e + d
            new[mid, :] = e
            if n < SUBCYCLES:
                fresh[ch] = (ahead(e), back(e))
            if lo + CHUNK > HALO and lo <= HALO + NJ:
                tail = float(TAIL_WEIGHTS[n - 1])
                if n == 1:
                    b_s[mid, :] = e
                    b_g[mid, :] = tail * e
                else:
                    b_s[mid, :] = b_s[mid, :] + e
                    b_g[mid, :] = b_g[mid, :] + tail * e
        turned = fresh

    mid = pl.ds(8 + HALO, NJ)
    above = pl.ds(9 + HALO, NJ)
    core = pl.ds(HALO, NJ)
    last = eta_bufs[SUBCYCLES % 2]
    flat_o[0] = last[mid, :].T[CORE]
    wu = b_wu[core, :] * 2.0
    wv = b_wv[mid, :] * 2.0
    pu, pv, u0, v0 = b_pu[core, :], b_pv[mid, :], b_u[core, :], b_v[mid, :]
    s, g = b_s[mid, :], b_g[mid, :]
    flat_o[1] = (u0 + SUBCYCLES * pu - wu * (ahead(s) - s)).T[CORE]
    flat_o[2] = (v0 + SUBCYCLES * pv - wv * (b_s[above, :] - s)).T[CORE]
    mean_u = u0 + MEAN_STEP * pu - wu * (ahead(g) - g)
    mean_v = v0 + MEAN_STEP * pv - wv * (b_g[above, :] - g)
    for f, (mean, depth_ref, km_ref) in enumerate(((mean_u, hu2, kmu), (mean_v, hv2, kmv))):
        d = depth_ref[...]
        flat_o[3 + f] = mean.T[CORE] / jnp.where(d > 0, d, 1.0) - smr[f]
        flat_o[5 + f] = km_ref[...]

    sent(g0 + g1, g2b_n, g2b_s)
    sent(g2, g3n + g5n + g7n, g3s + g5s + g7s)
    sent((), g2a_n + gc_n + gd_n, g2a_s + gc_s + gd_s)
    sent(g4, g4_n + g6_n, g4_s + g6_s)


CHUNKS = ((46, 62), (30, 46), (14, 30), (0, 14))


def back_kernel(du, dv, dt, ds, flat, eta_h, tu_h, tv_h, u_h, v_h, t_h, s_h, xu, xv, xt, xs, sem2, sem3):
    copies = [pltpu.make_async_copy(flat.at[f], out, sem2.at[f]) for f, out in enumerate((eta_h, tu_h, tv_h))]
    for cp in copies:
        cp.start()
    for n, (lo, hi) in enumerate(CHUNKS):
        def body(ib, carry):
            rows = pl.ds(pl.multiple_of(ib * 8, 8), 8)
            cu, cv, ku, kv = (flat[f, rows, :] for f in (3, 4, 5, 6))
            if hi == LEVELS:
                x = [jnp.zeros((8, NJ), F32) for _ in range(4)]
            else:
                x = [ref[rows, :] for ref in (carry_refs)]
            for k in range(hi - 1, lo - 1, -1):
                x[0] = du[k, rows, :] + RATIO_V[k] * x[0]
                x[1] = dv[k, rows, :] + RATIO_V[k] * x[1]
                x[2] = dt[k, rows, :] + RATIO_D[k] * x[2]
                x[3] = ds[k, rows, :] + RATIO_D[k] * x[3]
                xu[k, rows, :] = jnp.where(ku > k, x[0] + cu, 0.0)
                xv[k, rows, :] = jnp.where(kv > k, x[1] + cv, 0.0)
                xt[k, rows, :] = x[2]
                xs[k, rows, :] = x[3]
            for ref, val in zip(carry_refs, x):
                ref[rows, :] = val
            return carry
        carry_refs = (xu.at[LEVELS], xv.at[LEVELS], xt.at[LEVELS], xs.at[LEVELS])
        lax.fori_loop(0, NI // 8, body, 0)
        for f, (src, out) in enumerate(((xu, u_h), (xv, v_h), (xt, t_h), (xs, s_h))):
            cp = pltpu.make_async_copy(src.at[lo:hi], out.at[lo:hi], sem3.at[n, f])
            cp.start()
            copies.append(cp)
    for cp in copies:
        cp.wait()


def solution(mesh):
    col_count = mesh.shape['col']
    row_count = mesh.shape['row']

    def ocean_step(*args):
        flipped = [jnp.swapaxes(x, -1, -2) for x in args]
        cube = (LEVELS, NI, NJ)
        flat = (NI, NJ)
        dma = pltpu.SemaphoreType.DMA
        hbm = pl.BlockSpec(memory_space=pltpu.HBM)
        vmem = pl.BlockSpec(memory_space=VMEM)
        padded = VMEM((LEVELS, IPAD, NJ), F32)
        pair = VMEM((2,) + flat, F32)
        block = VMEM(cube, F32)
        near = VMEM((2, OFF, NJ), F32)
        wide = VMEM((JEXT + 16, IEXT), F32)
        plain = VMEM((JEXT, IEXT), F32)
        inner = pl.pallas_call(
            functools.partial(exchange_kernel, col_count, row_count),
            out_shape=tuple(VMEM(cube, F32) for _ in range(4)) + (VMEM((7,) + flat, F32),),
            in_specs=[hbm] * 9,
            out_specs=(vmem,) * 5,
            scratch_shapes=[
                padded, padded, padded, padded, padded, padded, block, block, padded, block, block,
                VMEM((5, NI + OFF, NJ), F32), near, near, VMEM(flat, jnp.int32), VMEM((5, IEXT, NJ), F32),
                pair, pair, VMEM((2, IEXT, NJ), F32), VMEM((2, IEXT, NJ), F32),
                VMEM((4,) + flat, F32), pair, pair,
                VMEM((2, IPAD, NJ), F32), VMEM((2, IPAD, NJ), F32), VMEM((8, IPAD, NJ), F32),
                pair, VMEM((2, IEXT, NJ), F32),
                VMEM((1,) + flat, F32), VMEM((1,) + flat, F32),
                VMEM((1, IEXT, NJ), F32), VMEM((1, IEXT, NJ), F32),
                VMEM(flat, F32), VMEM(flat, F32), VMEM(flat, F32),
                VMEM(flat, F32), VMEM(flat, F32), pair,
                wide, wide, plain, plain, plain, plain, wide, plain, wide, plain, wide, wide, wide,
                dma((4,)), dma((5,)), dma((MESSAGES,)), dma((MESSAGES,)),
            ],
            compiler_params=pltpu.CompilerParams(
                collective_id=0, has_side_effects=True, vmem_limit_bytes=54 * 2 ** 20),
        )(*flipped)
        spare = VMEM((LEVELS + 1,) + flat, F32)
        outs = pl.pallas_call(
            back_kernel,
            out_shape=tuple(jax.ShapeDtypeStruct(flat, F32) for _ in range(3))
            + tuple(jax.ShapeDtypeStruct(cube, F32) for _ in range(4)),
            in_specs=[vmem] * 5,
            out_specs=(hbm,) * 7,
            scratch_shapes=[spare, spare, spare, spare, dma((3,)), dma((4, 4))],
            compiler_params=pltpu.CompilerParams(vmem_limit_bytes=40 * 2 ** 20),
        )(*inner)
        return tuple(jnp.swapaxes(x, -1, -2) for x in outs)

    spec_3d = P(None, 'row', 'col')
    spec_2d = P('row', 'col')
    return jax.shard_map(ocean_step, mesh=mesh, in_specs=(spec_3d,) * 4 + (spec_2d,) * 5, out_specs=(spec_2d,) * 3 + (spec_3d,) * 4, check_vma=False)
```

profile of v0, /device:TPU:1, one launch (start us, length us, event | category | flops | bytes accessed | tf_op | source)
XLA Modules:
  0.0 31.1 jit_solution(12918717464822987782)
XLA Ops:
  0.6 26.6 %shard_map.144 = (f32[62,64,128]{2,1,0:T(8,128)S(1)}, f32[62,64,128]{2,1,0:T(8,128)S(1)}, f32[62,64,128]{2,1,0:T(8,128)S(1)}, f32[62,64,128]{2,1,0:T(8,128)S(1)}, f32[7,64,128]{2,1,0:T(8,128)S(1)}) custom-call(f32[62,64,128]{2,1,0:T(8,128)} %bitcast.16, f32[62,64,128]{2,1,0:T(8,128)} %bitcast.17, f32[62,64,128]{2,1,0:T(8,128)} %bitcast.18, ...), custom_call_target="tpu_custom_call" | custom-call | tf_op jit(solution)/shard_map/pallas_call | solution.py:655
  27.2 3.9 %shard_map.145 = (f32[64,128]{1,0:T(8,128)}, f32[64,128]{1,0:T(8,128)}, f32[64,128]{1,0:T(8,128)}, f32[62,64,128]{2,1,0:T(8,128)}, f32[62,64,128]{2,1,0:T(8,128)...) custom-call(f32[62,64,128]{2,1,0:T(8,128)S(1)} %get-tuple-element.19.du, f32[62,64,128]{2,1,0:T(8,128)S(1)} %get-tuple-element.20.dv, ...), custom_call_target="tpu_custom_call" | custom-call | tf_op jit(solution)/shard_map/pallas_call | solution.py:678
where the time goes:
time: 31.3 us; the launch traced here: 31.1 us
  Pallas kernels  30.5 us (97%)
  between operations  0.64 us (2%)
    pallas_call x1, Pallas kernels, ocean_step(): pl.pallas_call(functools.partial(exchange_kernel, col_count, row_count),...  26.6 us
    pallas_call x1, Pallas kernels, ocean_step(): pl.pallas_call(back_kernel, out_shape=tuple((jax.ShapeDtypeStruct(flat, F...  3.9 us

commit v1 on v0

--- a/solution.py
+++ b/solution.py
@@ -63,7 +63,10 @@
 WEIGHTS = sm_weights()
 TAIL_WEIGHTS = np.cumsum(WEIGHTS[::-1])[::-1]
 MEAN_STEP = float(np.sum(WEIGHTS * np.arange(1, SUBCYCLES + 1)))
-MESSAGES = 38
+MESSAGES = 32
+PARTS = ((0, 16), (16, 32), (32, 48), (48, LEVELS))
+SPARE = 2 * LEVELS
+LAG_M = 2
 LAG = 7
 CHUNK = 24
 
@@ -97,7 +100,8 @@
     return x / jnp.maximum(count, 1.0)
 
 
-ETA, TU, TV, DEP, KMT = range(5)
+ETA, TU, TV, WET_DEP = range(4)
+DEP, KMT = range(2)
 U, V, T, S, MEAN, PRES, T_FLUX, S_FLUX = range(8)
 UV, TS = range(2)
 
@@ -106,7 +110,7 @@
     col_count, row_count,
     u_hbm, v_hbm, t_hbm, s_hbm, eta_hbm, tu_hbm, tv_hbm, dep_hbm, kmt_hbm,
     du_o, dv_o, dt_o, ds_o, flat_o,
-    u3, v3, t3, s3, p3, un3, us3, vn3, vs3, tn3, sn3, st2, near_w, near_e, kmt_i, ext2, pk2n, pk2s, hs2, hn2,
+    u3, v3, t3, s3, p3, un3, us3, vn3, vs3, tn3, sn3, st2, nd2, near_w, near_e, kmt_i, ext2, pk2n, pk2s, hs2, hn2,
     pack, mn, ms, in_s, in_n, rr,
     ff, extf, pkfn, pkfs, hsf, hnf,
     kmu, kmw, kmv, hu2, hv2, smr,
@@ -141,14 +145,21 @@
             greet(cc, down)
 
     loads2 = []
-    for f, src in enumerate((eta_hbm, tu_hbm, tv_hbm, dep_hbm)):
-        loads2.append(pltpu.make_async_copy(src, st2.at[f, :NI, :], ld2.at[f]))
-    loads2.append(pltpu.make_async_copy(kmt_hbm, kmt_i, ld2.at[KMT]))
+    for f, (src, dst) in enumerate((
+            (eta_hbm, st2.at[ETA]), (tu_hbm, st2.at[TU]), (tv_hbm, st2.at[TV]),
+            (dep_hbm, nd2.at[DEP, :NI, :]), (kmt_hbm, kmt_i))):
+        loads2.append(pltpu.make_async_copy(src, dst, ld2.at[f]))
     loads3 = []
     for f, (src, dst) in enumerate(((t_hbm, t3), (s_hbm, s3), (u_hbm, u3), (v_hbm, v3))):
-        loads3.append(pltpu.make_async_copy(src, dst.at[:, OWN, :], ld3.at[f]))
-    for cp in loads2 + loads3[:2]:
+        loads3.append([
+            pltpu.make_async_copy(src.at[lo:hi], dst.at[lo:hi, OWN, :], ld3.at[f, n])
+            for n, (lo, hi) in enumerate(PARTS)])
+    for cp in loads3[0] + loads2 + sum(loads3[1:], []):
         cp.start()
+
+    def landed(f):
+        for cp in loads3[f]:
+            cp.wait()
 
     def remote(src, dst, cc, row):
         n = next(label)
@@ -216,25 +227,11 @@
         top = jnp.zeros((NI, NJ), F32)
         bot = jnp.zeros((NI, NJ), F32)
         for q, f in enumerate(fields):
-            x = src[f, :NI, :]
+            x = src[f]
             top = jnp.where(group64 == q, rot(x, HALO * q + HALO), top)
             bot = jnp.where(group64 == q, rot(x, HALO * q), bot)
         pn[...] = top
         ps[...] = bot
-
-    for cp in loads2:
-        cp.wait()
-    for cp in loads3[2:]:
-        cp.start()
-    st2[KMT, :NI, :] = kmt_i[...].astype(F32)
-    for f in (DEP, KMT):
-        st2[f, NI:, :] = jnp.zeros((OFF, NJ), F32)
-    near2 = pk2n.at[1], pk2s.at[1], hs2.at[1], hn2.at[1]
-    far2 = pk2n.at[0], pk2s.at[0], hs2.at[0], hn2.at[0]
-    pack_flat((DEP, KMT), st2, *near2[:2])
-    pack_flat((ETA, TU, TV), st2, *far2[:2])
-    for f in range(5):
-        ext2[f, CORE, :] = st2[f, :NI, :]
 
     lane8 = lax.broadcasted_iota(jnp.int32, (8, NJ), 1)
     first8 = lane8 == 0
@@ -253,47 +250,63 @@
 
     def pack_pair(a):
         x, y = pack[2 * a], pack[2 * a + 1]
-        mn[a] = jnp.where(even64, y, back(x))
-        ms[a] = jnp.where(even64, ahead(x), y)
-
-    loads3[0].wait()
+        return jnp.where(even64, y, back(x)), jnp.where(even64, ahead(x), y)
+
+    def with_near(top, bottom):
+        for f in (DEP, KMT):
+            x = nd2[f, :NI, :]
+            spare = lane64 == SPARE + f
+            top = jnp.where(spare, rot(x, SPARE + f + 1), top)
+            bottom = jnp.where(spare, rot(x, SPARE + f), bottom)
+        return top, bottom
+
+    landed(0)
     pack_edges(T, t3)
+    for cp in loads2:
+        cp.wait()
+    kmt = kmt_i[...].astype(F32)
+    nd2[KMT, :NI, :] = kmt
+    nd2[:, NI:, :] = jnp.zeros((2, OFF, NJ), F32)
+    st2[WET_DEP] = keep(kmt > 0, nd2[DEP, :NI, :])
 
     pl.semaphore_wait(barrier, 2 + 3 * has_n.astype(jnp.int32) + 3 * has_s.astype(jnp.int32))
     g0 = [
-        remote(st2.at[DEP:KMT + 1, EAST, :], near_w.at[:, WEST, :], east, r),
-        remote(st2.at[DEP:KMT + 1, WEST, :], near_e.at[:, WEST, :], west, r),
+        remote(nd2.at[:, EAST, :], near_w.at[:, WEST, :], east, r),
+        remote(nd2.at[:, WEST, :], near_e.at[:, WEST, :], west, r),
     ]
-    g2b_n, g2b_s = near_ns(*near2)
-    start(g0 + g1, g2b_n, g2b_s)
-
-    loads3[1].wait()
+    start(g0 + g1)
+
+    landed(1)
     pack_edges(S, s3)
-    pack_pair(TS)
+    mn[TS], ms[TS] = with_near(*pack_pair(TS))
     g3n, g3s = near_ns(mn.at[TS], ms.at[TS], in_s.at[TS, OWN, :], in_n.at[TS, OWN, :])
     start((), g3n, g3s)
-    loads3[2].wait()
+    landed(2)
     pack_edges(U, u3)
-    loads3[3].wait()
+    landed(3)
     pack_edges(V, v3)
-    pack_pair(UV)
+    mn[UV], ms[UV] = pack_pair(UV)
     g5n, g5s = near_ns(mn.at[UV], ms.at[UV], in_s.at[UV, OWN, :], in_n.at[UV, OWN, :])
     g7n = [remote(mn.at[UV, :OFF, :], in_s.at[UV, AFTER, :], west, up)]
     g7s = [remote(ms.at[UV, NI - OFF:NI, :], in_n.at[UV, BEFORE, :], east, down)]
     start((), g5n + g7n, g5s + g7s)
+    wide2 = pk2n.at[0], pk2s.at[0], hs2.at[0], hn2.at[0]
+    pack_flat(range(4), st2, *wide2[:2])
     g2 = side_ew(st2, ext2)
-    g2a_n, g2a_s = near_ns(*far2)
-    gc_n, gc_s = corners(*near2)
-    gd_n, gd_s = corners(*far2)
-    start(g2, g2a_n + gc_n + gd_n, g2a_s + gc_s + gd_s)
+    g2a_n, g2a_s = near_ns(*wide2)
+    gc_n, gc_s = corners(*wide2)
+    start(g2, g2a_n + gc_n, g2a_s + gc_s)
+    for f in range(4):
+        ext2[f, CORE, :] = st2[f]
 
     def local_body(ib, carry):
         mid, at = rows(ib, OFF), rows(ib)
-        km = st2[KMT, at, :]
-        thick = per_level(st2[DEP, at, :], km)
+        km = nd2[KMT, at, :]
+        thick = 2.0 * per_level(nd2[DEP, at, :], km)
         total = jnp.zeros((8, NJ), F32)
         for k in range(LEVELS):
             u, v = u3[k, mid, :], v3[k, mid, :]
+            u = 0.25 * u
             un3[k, mid, :] = ahead(u)
             us3[k, at, :] = back(u)
             vn3[k, at, :] = ahead(v)
@@ -305,16 +318,15 @@
     blocks = NI // 8
     lax.fori_loop(0, blocks, local_body, 0)
 
-    recv((), g2b_n, g2b_s)
+    recv((), g3n, g3s)
     has_nf = keep(has_n, 1.0).astype(F32)
     has_sf = keep(has_s, 1.0).astype(F32)
     big_n = jnp.full((NI, 1), has_nf) > 0.5
     big_s = jnp.full((NI, 1), has_sf) > 0.5
-    kmt = st2[KMT, :NI, :]
-    depth = st2[DEP, :NI, :]
-    dep_n = keep(big_n, hn2[1, CORE, 0:1])
-    kmt_n = keep(big_n, hn2[1, CORE, HALO:HALO + 1])
-    kmt_s = keep(big_s, hs2[1, CORE, 2 * HALO - 1:2 * HALO])
+    depth = nd2[DEP, :NI, :]
+    dep_n = keep(big_n, in_n[TS, OWN, SPARE + DEP:SPARE + DEP + 1])
+    kmt_n = keep(big_n, in_n[TS, OWN, SPARE + KMT:SPARE + KMT + 1])
+    kmt_s = keep(big_s, in_s[TS, OWN, SPARE + KMT:SPARE + KMT + 1])
     last64 = lane64 == NJ - 1
     kmt_north = jnp.where(last64, kmt_n, ahead(kmt))
     dep_north = jnp.where(last64, dep_n, ahead(depth))
@@ -323,9 +335,9 @@
     hv2[...] = keep(kmv_v > 0, 0.5 * (depth + dep_north))
 
     def u_faces():
-        kmu_v = jnp.minimum(st2[KMT, :NI, :], st2[KMT, 1:NI + 1, :])
+        kmu_v = jnp.minimum(nd2[KMT, :NI, :], nd2[KMT, 1:NI + 1, :])
         kmu[...] = kmu_v
-        hu2[...] = keep(kmu_v > 0, 0.5 * (st2[DEP, :NI, :] + st2[DEP, 1:NI + 1, :]))
+        hu2[...] = keep(kmu_v > 0, 0.5 * (nd2[DEP, :NI, :] + nd2[DEP, 1:NI + 1, :]))
 
     u_faces()
 
@@ -333,7 +345,8 @@
         north = keep(has_nf > 0.5, in_n[a, where, :])
         south = keep(has_sf > 0.5, in_s[a, where, :])
         even = (lax.broadcasted_iota(jnp.int32, north.shape, 1) & 1) == 0
-        rr[2 * a, where, :] = jnp.where(even, north, south)
+        first = jnp.where(even, north, south)
+        rr[2 * a, where, :] = 0.25 * first if a == UV else first
         rr[2 * a + 1, where, :] = jnp.where(even, ahead(north), back(south))
 
     def mean_rows():
@@ -341,13 +354,12 @@
         mean_s = rr[V, OWN, :] + rr[V, OFF + 1:OFF + NI + 1, :]
         rr[MEAN, OWN, :] = jnp.where(even64, mean_n, mean_s)
 
-    recv((), g3n, g3s)
     unpack_pair(TS, OWN)
     rt, rs = rr[T, OWN, :], rr[S, OWN, :]
     dens = keep((kmt_n > slot64.astype(F32)) & even64, BETA_S * rs - ALPHA_T * rt)
     above = lax.broadcasted_iota(jnp.int32, (NJ, NJ), 0) <= lax.broadcasted_iota(jnp.int32, (NJ, NJ), 1)
     total = jnp.dot(dens, above.astype(F32), precision=lax.Precision.HIGHEST, preferred_element_type=F32)
-    rr[PRES, OWN, :] = (total - 0.5 * dens) * per_level(dep_n, kmt_n)
+    rr[PRES, OWN, :] = (total - 0.5 * dens) * (2.0 * per_level(dep_n, kmt_n))
     recv((), g5n, g5s)
     rr[U, BEFORE, :] = jnp.zeros((OFF, NJ), F32)
     rr[V, AFTER, :] = jnp.zeros((OFF, NJ), F32)
@@ -367,9 +379,20 @@
         qu, qv, qm, qp = (rr[f, mid, :] for f in (U, V, MEAN, PRES))
         zero = jnp.zeros((8, NJ), F32)
         du, dv, st_u, st_v, sr_u, sr_v = (zero,) * 6
-        for k in range(LEVELS):
-            sh = NJ - 1 - 2 * k
-            hu, hv, hm, hp = rot(qu, sh), rot(qv, sh), rot(qm, sh), rot(qp, sh)
+        turned = {}
+        for step in range(LEVELS + LAG_M):
+            k = step
+            if k < LEVELS:
+                sh = NJ - 1 - 2 * k
+                turned[k] = (
+                    rot(qu, sh), rot(qv, sh), rot(qm, sh), rot(qp, sh),
+                    ahead(p3[k, mid, :]), ahead(t3[k, mid, :]), ahead(s3[k, mid, :]))
+            k = step - LAG_M
+            if k < 0:
+                continue
+            hu, hv, hm, hp, p_next, t_next, s_next = turned.pop(k)
+            tn3[k, at, :] = t_next
+            sn3[k, at, :] = s_next
             u = u3[k, mid, :]
             ue = u3[k, above, :]
             uw = u3[k, below, :]
@@ -384,54 +407,45 @@
             vn = jnp.where(last8, hv, vn3[k, at, :])
             vs = jnp.where(first8, hv, vs_k)
             vm4 = (v + ve) + jnp.where(first8, hm, vs_k + vs3[k, above, :])
-            um4 = (u + uw) + jnp.where(last8, hm, un_k + un3[k, below, :])
-            pn = jnp.where(last8, hp, ahead(p))
-            tn3[k, at, :] = ahead(t3[k, mid, :])
-            sn3[k, at, :] = ahead(s3[k, mid, :])
-            tu = (p - pe) - 0.5 * (u * (ue - uw)) - 0.125 * (vm4 * (un - us))
-            tv = (p - pn) - 0.125 * (um4 * (ve - vw)) - 0.5 * (v * (vn - vs))
+            um = 0.25 * (u + uw) + jnp.where(last8, hm, un_k + un3[k, below, :])
+            pn = jnp.where(last8, hp, p_next)
+            tu = (p - pe) - u * (ue - uw) - vm4 * (un - us)
+            tv = (p - pn) - um * (ve - vw) - v * (vn - vs)
             wu = km_u > k
             wv = km_v > k
-            tu = keep(wu, tu)
-            tv = keep(wv, tv)
-            ru_k = keep(wu, u) + ADV_COURANT * tu
-            rv_k = keep(wv, v) + ADV_COURANT * tv
-            st_u = st_u + tu
-            st_v = st_v + tv
-            sr_u = sr_u + ru_k
-            sr_v = sr_v + rv_k
-            fu = jnp.where(km_u > k + 1, INNER_V[k], keep(wu, LAST_V[k]))
-            fv = jnp.where(km_v > k + 1, INNER_V[k], keep(wv, LAST_V[k]))
-            if k > 0:
-                ru_k = ru_k + VISC_NUM * du
-                rv_k = rv_k + VISC_NUM * dv
-            du = ru_k * fu
-            dv = rv_k * fv
+            st_u = st_u + keep(wu, tu)
+            st_v = st_v + keep(wv, tv)
+            ru_k = u + (0.5 * ADV_COURANT) * tu
+            rv_k = v + (0.5 * ADV_COURANT) * tv
+            sr_u = sr_u + keep(wu, ru_k)
+            sr_v = sr_v + keep(wv, rv_k)
+            du = ru_k + RATIO_V[k - 1] * du if k else ru_k
+            dv = rv_k + RATIO_V[k - 1] * dv if k else rv_k
             du_o[k, at, :] = du
             dv_o[k, at, :] = dv
         inv_u = per_level(1.0, km_u)
         inv_v = per_level(1.0, km_v)
-        ff[0, at, :] = hu2[at, :] * inv_u * st_u
-        ff[1, at, :] = hv2[at, :] * inv_v * st_v
+        ff[0, at, :] = hu2[at, :] * inv_u * (0.5 * st_u)
+        ff[1, at, :] = hv2[at, :] * inv_v * (0.5 * st_v)
         smr[0, at, :] = inv_u * sr_u
         smr[1, at, :] = inv_v * sr_v
 
     def beside():
         recv(g0 + g1, g7n, g7s)
-        for n, f in enumerate((DEP, KMT)):
-            st2[f, NI:NI + 1, :] = near_e[n, WEST, :]
+        for f in (DEP, KMT):
+            nd2[f, NI:NI + 1, :] = near_e[f, WEST, :]
         u_faces()
-        kmt = st2[KMT, :NI, :]
+        kmt = nd2[KMT, :NI, :]
         first_col = lax.broadcasted_iota(jnp.int32, (NI, NJ), 0) == 0
-        kmw[...] = jnp.minimum(kmt, jnp.where(first_col, near_w[1, WEST, :], pltpu.roll(kmt, 1, 0)))
+        kmw[...] = jnp.minimum(kmt, jnp.where(first_col, near_w[KMT, WEST, :], pltpu.roll(kmt, 1, 0)))
         unpack_pair(UV, BEFORE)
         unpack_pair(UV, AFTER)
         mean_rows()
-        km_e = near_e[1, WEST, :]
-        thick_e = per_level(near_e[0, WEST, :], km_e)
+        km_e = near_e[KMT, WEST, :]
+        thick_e = 2.0 * per_level(near_e[DEP, WEST, :], km_e)
         tot_e = jnp.zeros((1, NJ), F32)
         for k in range(LEVELS):
-            un3[k, WEST_HALO, :] = ahead(u3[k, WEST_HALO, :])
+            un3[k, WEST_HALO, :] = ahead(0.25 * u3[k, WEST_HALO, :])
             vs3[k, EAST_HALO, :] = back(v3[k, EAST_HALO, :])
             dens_e = keep(km_e > k, BETA_S * s3[k, EAST_HALO, :] - ALPHA_T * t3[k, EAST_HALO, :])
             tot_e = tot_e + dens_e
@@ -457,7 +471,6 @@
         km_u = kmu[at, :]
         km_w = kmw[at, :]
         km_v = kmv[at, :]
-        km = st2[KMT, at, :]
         fields = ((t3, tn3, rr[T_FLUX, mid, :], dt_o), (s3, sn3, rr[S_FLUX, mid, :], ds_o))
         prev = [None, None]
         turned, flux = {}, {}
@@ -469,32 +482,28 @@
             k = step - LAG
             if 0 <= k < LEVELS:
                 v = keep(km_v > k, v3[k, mid, :])
-                v_pos, v_neg = pos(v), neg(v)
+                northward = v > 0
                 flux[k] = []
                 for (ref, next_ref, _, _), (north, south) in zip(fields, turned.pop(k)):
                     xn = jnp.where(last8, north, next_ref[k, at, :])
-                    fn = v_pos * ref[k, mid, :] + v_neg * xn
+                    fn = v * jnp.where(northward, ref[k, mid, :], xn)
                     flux[k].append((fn, back(jnp.where(last8, south, fn))))
             k = step - 2 * LAG
             if k >= 0:
                 u = keep(km_u > k, u3[k, mid, :])
                 w = keep(km_w > k, u3[k, below, :])
-                u_pos, u_neg = pos(u), neg(u)
-                w_pos, w_neg = pos(w), neg(w)
-                fac = jnp.where(km > k + 1, INNER_D[k], keep(km > k, LAST_D[k]))
+                eastward, from_west = u > 0, w > 0
                 for n, ((ref, _, _, out), (fn, fs)) in enumerate(zip(fields, flux.pop(k))):
                     x = ref[k, mid, :]
-                    fe = u_pos * x + u_neg * ref[k, above, :]
-                    fw = w_pos * ref[k, below, :] + w_neg * x
+                    fe = u * jnp.where(eastward, x, ref[k, above, :])
+                    fw = w * jnp.where(from_west, ref[k, below, :], x)
                     rhs = x - ADV_COURANT * ((fe - fw) + (fn - fs))
-                    if k > 0:
-                        rhs = rhs + DIFF_NUM * prev[n]
-                    prev[n] = rhs * fac
+                    prev[n] = rhs + RATIO_D[k - 1] * prev[n] if k else rhs
                     out[k, at, :] = prev[n]
         return carry
     lax.fori_loop(0, blocks, tracer_body, 0)
 
-    recv(g2, g2a_n + gc_n + gd_n, g2a_s + gc_s + gd_s)
+    recv(g2, g2a_n + gc_n, g2a_s + gc_s)
     low_ok = jnp.full((HALO, IEXT), has_sf) > 0.5
     high_ok = jnp.full((HALO, IEXT), has_nf) > 0.5
 
@@ -503,8 +512,7 @@
         high = keep(high_ok, hn[HALO * q:HALO * (q + 1)])
         return jnp.concatenate([low, ext.T, high], axis=0)
 
-    hs_t = [hs2[a].T for a in range(2)]
-    hn_t = [hn2[a].T for a in range(2)]
+    hs_t, hn_t = hs2[0].T, hn2[0].T
     win = pl.ds(8, JEXT)
     north_of = pl.ds(9, JEXT)
     south_of = pl.ds(7, JEXT)
@@ -512,20 +520,19 @@
     for ref in (b_e0, b_e1, b_wv, b_v, b_pv, b_s, b_g):
         ref[0:8, :] = zpad
         ref[8 + JEXT:16 + JEXT, :] = zpad
-    b_s[win, :] = window(ext2[KMT], hs_t[1], hn_t[1], 1)
-    b_g[win, :] = window(ext2[DEP], hs_t[1], hn_t[1], 0)
-    km_w = b_s[win, :]
-    dp_w = b_g[win, :]
-    wet_u = jnp.minimum(km_w, ahead(km_w)) > 0
-    wet_v = jnp.minimum(km_w, b_s[north_of, :]) > 0
-    wu = keep(wet_u, (0.25 * WAVE_COURANT) * (dp_w + ahead(dp_w)))
-    wv = keep(wet_v, (0.25 * WAVE_COURANT) * (dp_w + b_g[north_of, :]))
+    dp_w = window(ext2[WET_DEP], hs_t, hn_t, WET_DEP)
+    b_s[win, :] = dp_w
+    dp_n, dp_e = b_s[north_of, :], ahead(dp_w)
+    wet_u = (dp_w > 0) & (dp_e > 0)
+    wet_v = (dp_w > 0) & (dp_n > 0)
+    wu = keep(wet_u, (0.25 * WAVE_COURANT) * (dp_w + dp_e))
+    wv = keep(wet_v, (0.25 * WAVE_COURANT) * (dp_w + dp_n))
     b_wu[...] = wu
     b_ww[...] = back(wu)
     b_wv[win, :] = wv
-    b_e0[win, :] = keep(km_w > 0, window(ext2[ETA], hs_t[0], hn_t[0], ETA))
-    u0 = keep(wet_u, window(ext2[TU], hs_t[0], hn_t[0], TU))
-    v0 = keep(wet_v, window(ext2[TV], hs_t[0], hn_t[0], TV))
+    b_e0[win, :] = keep(dp_w > 0, window(ext2[ETA], hs_t, hn_t, ETA))
+    u0 = keep(wet_u, window(ext2[TU], hs_t, hn_t, TU))
+    v0 = keep(wet_v, window(ext2[TV], hs_t, hn_t, TV))
     b_u[...] = u0
     b_v[win, :] = v0
     b_d[...] = -WAVE_COURANT * ((u0 - back(u0)) + (v0 - b_v[south_of, :]))
@@ -591,43 +598,45 @@
         d = depth_ref[...]
         flat_o[3 + f] = mean.T[CORE] / jnp.where(d > 0, d, 1.0) - smr[f]
         flat_o[5 + f] = km_ref[...]
-
-    sent(g0 + g1, g2b_n, g2b_s)
+    flat_o[7] = nd2[KMT, :NI, :]
+
+    sent(g0 + g1)
     sent(g2, g3n + g5n + g7n, g3s + g5s + g7s)
-    sent((), g2a_n + gc_n + gd_n, g2a_s + gc_s + gd_s)
+    sent((), g2a_n + gc_n, g2a_s + gc_s)
     sent(g4, g4_n + g6_n, g4_s + g6_s)
 
 
-CHUNKS = ((46, 62), (30, 46), (14, 30), (0, 14))
+CHUNKS = ((54, 62), (42, 54), (28, 42), (14, 28), (0, 14))
 
 
 def back_kernel(du, dv, dt, ds, flat, eta_h, tu_h, tv_h, u_h, v_h, t_h, s_h, xu, xv, xt, xs, sem2, sem3):
     copies = [pltpu.make_async_copy(flat.at[f], out, sem2.at[f]) for f, out in enumerate((eta_h, tu_h, tv_h))]
     for cp in copies:
         cp.start()
+    results = ((xu, u_h), (xv, v_h), (xt, t_h), (xs, s_h))
     for n, (lo, hi) in enumerate(CHUNKS):
         def body(ib, carry):
             rows = pl.ds(pl.multiple_of(ib * 8, 8), 8)
-            cu, cv, ku, kv = (flat[f, rows, :] for f in (3, 4, 5, 6))
-            if hi == LEVELS:
-                x = [jnp.zeros((8, NJ), F32) for _ in range(4)]
-            else:
-                x = [ref[rows, :] for ref in (carry_refs)]
+            cu, cv, ku, kv, kt = (flat[f, rows, :] for f in range(3, 8))
+            x = [jnp.zeros((8, NJ), F32) if hi == LEVELS else ref[LEVELS, rows, :] for ref, _ in results]
             for k in range(hi - 1, lo - 1, -1):
-                x[0] = du[k, rows, :] + RATIO_V[k] * x[0]
-                x[1] = dv[k, rows, :] + RATIO_V[k] * x[1]
-                x[2] = dt[k, rows, :] + RATIO_D[k] * x[2]
-                x[3] = ds[k, rows, :] + RATIO_D[k] * x[3]
-                xu[k, rows, :] = jnp.where(ku > k, x[0] + cu, 0.0)
-                xv[k, rows, :] = jnp.where(kv > k, x[1] + cv, 0.0)
+                wu, wv = ku > k, kv > k
+                fu = jnp.where(ku > k + 1, INNER_V[k], keep(wu, LAST_V[k]))
+                fv = jnp.where(kv > k + 1, INNER_V[k], keep(wv, LAST_V[k]))
+                ft = jnp.where(kt > k + 1, INNER_D[k], keep(kt > k, LAST_D[k]))
+                x[0] = fu * du[k, rows, :] + RATIO_V[k] * x[0]
+                x[1] = fv * dv[k, rows, :] + RATIO_V[k] * x[1]
+                x[2] = ft * dt[k, rows, :] + RATIO_D[k] * x[2]
+                x[3] = ft * ds[k, rows, :] + RATIO_D[k] * x[3]
+                xu[k, rows, :] = keep(wu, x[0] + cu)
+                xv[k, rows, :] = keep(wv, x[1] + cv)
                 xt[k, rows, :] = x[2]
                 xs[k, rows, :] = x[3]
-            for ref, val in zip(carry_refs, x):
-                ref[rows, :] = val
+            for (ref, _), val in zip(results, x):
+                ref[LEVELS, rows, :] = val
             return carry
-        carry_refs = (xu.at[LEVELS], xv.at[LEVELS], xt.at[LEVELS], xs.at[LEVELS])
         lax.fori_loop(0, NI // 8, body, 0)
-        for f, (src, out) in enumerate(((xu, u_h), (xv, v_h), (xt, t_h), (xs, s_h))):
+        for f, (src, out) in enumerate(results):
             cp = pltpu.make_async_copy(src.at[lo:hi], out.at[lo:hi], sem3.at[n, f])
             cp.start()
             copies.append(cp)
@@ -649,27 +658,28 @@
         padded = VMEM((LEVELS, IPAD, NJ), F32)
         pair = VMEM((2,) + flat, F32)
         block = VMEM(cube, F32)
+        single = VMEM((1,) + flat, F32)
         near = VMEM((2, OFF, NJ), F32)
         wide = VMEM((JEXT + 16, IEXT), F32)
         plain = VMEM((JEXT, IEXT), F32)
         inner = pl.pallas_call(
             functools.partial(exchange_kernel, col_count, row_count),
-            out_shape=tuple(VMEM(cube, F32) for _ in range(4)) + (VMEM((7,) + flat, F32),),
+            out_shape=tuple(VMEM(cube, F32) for _ in range(4)) + (VMEM((8,) + flat, F32),),
             in_specs=[hbm] * 9,
             out_specs=(vmem,) * 5,
             scratch_shapes=[
                 padded, padded, padded, padded, padded, padded, block, block, padded, block, block,
-                VMEM((5, NI + OFF, NJ), F32), near, near, VMEM(flat, jnp.int32), VMEM((5, IEXT, NJ), F32),
-                pair, pair, VMEM((2, IEXT, NJ), F32), VMEM((2, IEXT, NJ), F32),
+                VMEM((4,) + flat, F32), VMEM((2, NI + OFF, NJ), F32), near, near, VMEM(flat, jnp.int32),
+                VMEM((4, IEXT, NJ), F32), single, single, VMEM((1, IEXT, NJ), F32), VMEM((1, IEXT, NJ), F32),
                 VMEM((4,) + flat, F32), pair, pair,
                 VMEM((2, IPAD, NJ), F32), VMEM((2, IPAD, NJ), F32), VMEM((8, IPAD, NJ), F32),
                 pair, VMEM((2, IEXT, NJ), F32),
-                VMEM((1,) + flat, F32), VMEM((1,) + flat, F32),
+                single, single,
                 VMEM((1, IEXT, NJ), F32), VMEM((1, IEXT, NJ), F32),
                 VMEM(flat, F32), VMEM(flat, F32), VMEM(flat, F32),
                 VMEM(flat, F32), VMEM(flat, F32), pair,
                 wide, wide, plain, plain, plain, plain, wide, plain, wide, plain, wide, wide, wide,
-                dma((4,)), dma((5,)), dma((MESSAGES,)), dma((MESSAGES,)),
+                dma((4, len(PARTS))), dma((5,)), dma((MESSAGES,)), dma((MESSAGES,)),
             ],
             compiler_params=pltpu.CompilerParams(
                 collective_id=0, has_side_effects=True, vmem_limit_bytes=54 * 2 ** 20),
@@ -681,7 +691,7 @@
             + tuple(jax.ShapeDtypeStruct(cube, F32) for _ in range(4)),
             in_specs=[vmem] * 5,
             out_specs=(hbm,) * 7,
-            scratch_shapes=[spare, spare, spare, spare, dma((3,)), dma((4, 4))],
+            scratch_shapes=[spare, spare, spare, spare, dma((3,)), dma((len(CHUNKS), 4))],
             compiler_params=pltpu.CompilerParams(vmem_limit_bytes=40 * 2 ** 20),
         )(*inner)
         return tuple(jnp.swapaxes(x, -1, -2) for x in outs)

time: 31.3 us -> 30.9 us (0.987)
  Pallas kernels: 30.5 us -> 30.1 us
where the time goes in v1:
time: 30.9 us; the launch traced here: 30.7 us
  Pallas kernels  30.1 us (97%)
  between operations  0.64 us (2%)
    pallas_call x1, Pallas kernels, ocean_step(): pl.pallas_call(functools.partial(exchange_kernel, col_count, row_count),...  26.3 us
    pallas_call x1, Pallas kernels, ocean_step(): pl.pallas_call(back_kernel, out_shape=tuple((jax.ShapeDtypeStruct(flat, F...  3.79 us

profile of v1, /device:TPU:1, one launch (start us, length us, event | category | flops | bytes accessed | tf_op | source)
XLA Modules:
  0.0 30.7 jit_solution(16381456007681568671)
XLA Ops:
  0.6 26.3 %shard_map.144 = (f32[62,64,128]{2,1,0:T(8,128)S(1)}, f32[62,64,128]{2,1,0:T(8,128)S(1)}, f32[62,64,128]{2,1,0:T(8,128)S(1)}, f32[62,64,128]{2,1,0:T(8,128)S(1)}, f32[8,64,128]{2,1,0:T(8,128)S(1)}) custom-call(f32[62,64,128]{2,1,0:T(8,128)} %bitcast.16, f32[62,64,128]{2,1,0:T(8,128)} %bitcast.17, f32[62,64,128]{2,1,0:T(8,128)} %bitcast.18, ...), custom_call_target="tpu_custom_call" | custom-call | tf_op jit(solution)/shard_map/pallas_call | solution.py:665
  26.9 3.8 %shard_map.145 = (f32[64,128]{1,0:T(8,128)}, f32[64,128]{1,0:T(8,128)}, f32[64,128]{1,0:T(8,128)}, f32[62,64,128]{2,1,0:T(8,128)}, f32[62,64,128]{2,1,0:T(8,128)...) custom-call(f32[62,64,128]{2,1,0:T(8,128)S(1)} %get-tuple-element.19.du, f32[62,64,128]{2,1,0:T(8,128)S(1)} %get-tuple-element.20.dv, ...), custom_call_target="tpu_custom_call" | custom-call | tf_op jit(solution)/shard_map/pallas_call | solution.py:688

commit v2 on v1

--- a/solution.py
+++ b/solution.py
@@ -64,10 +64,12 @@
 TAIL_WEIGHTS = np.cumsum(WEIGHTS[::-1])[::-1]
 MEAN_STEP = float(np.sum(WEIGHTS * np.arange(1, SUBCYCLES + 1)))
 MESSAGES = 32
+STAGGER = 500
+TALL = 16
 PARTS = ((0, 16), (16, 32), (32, 48), (48, LEVELS))
 SPARE = 2 * LEVELS
 LAG_M = 2
-LAG = 7
+LAG = 4
 CHUNK = 24
 
 
@@ -154,12 +156,22 @@
         loads3.append([
             pltpu.make_async_copy(src.at[lo:hi], dst.at[lo:hi, OWN, :], ld3.at[f, n])
             for n, (lo, hi) in enumerate(PARTS)])
-    for cp in loads3[0] + loads2 + sum(loads3[1:], []):
-        cp.start()
+
+    def fetch(f):
+        for cp in loads3[f]:
+            cp.start()
 
     def landed(f):
         for cp in loads3[f]:
             cp.wait()
+
+    fetch(0)
+    for cp in loads2:
+        cp.start()
+    pl.delay(STAGGER)
+    fetch(1)
+    pl.delay(STAGGER)
+    fetch(2)
 
     def remote(src, dst, cc, row):
         n = next(label)
@@ -239,8 +251,12 @@
     slot64 = lane64 >> 1
     even64 = (lane64 & 1) == 0
 
-    def rows(ib, off=0):
-        return pl.ds(pl.multiple_of(ib * 8, 8) + off, 8)
+    def rows(ib, off=0, size=8):
+        return pl.ds(pl.multiple_of(ib * size, 8) + off, size)
+
+    def edge_lanes(size):
+        lane = lax.broadcasted_iota(jnp.int32, (size, NJ), 1)
+        return lane == 0, lane == NJ - 1
 
     def pack_edges(f, ref):
         acc = jnp.zeros((NI, NJ), F32)
@@ -262,6 +278,7 @@
 
     landed(0)
     pack_edges(T, t3)
+    fetch(3)
     for cp in loads2:
         cp.wait()
     kmt = kmt_i[...].astype(F32)
@@ -300,10 +317,10 @@
         ext2[f, CORE, :] = st2[f]
 
     def local_body(ib, carry):
-        mid, at = rows(ib, OFF), rows(ib)
+        mid, at = rows(ib, OFF, TALL), rows(ib, 0, TALL)
         km = nd2[KMT, at, :]
         thick = 2.0 * per_level(nd2[DEP, at, :], km)
-        total = jnp.zeros((8, NJ), F32)
+        total = jnp.zeros((TALL, NJ), F32)
         for k in range(LEVELS):
             u, v = u3[k, mid, :], v3[k, mid, :]
             u = 0.25 * u
@@ -316,7 +333,7 @@
             p3[k, mid, :] = (total - 0.5 * dens) * thick
         return carry
     blocks = NI // 8
-    lax.fori_loop(0, blocks, local_body, 0)
+    lax.fori_loop(0, NI // TALL, local_body, 0)
 
     recv((), g3n, g3s)
     has_nf = keep(has_n, 1.0).astype(F32)
@@ -467,7 +484,9 @@
         extf[f, CORE, :] = ff[f]
 
     def tracer_body(ib, carry):
-        at, mid, below, above = rows(ib), rows(ib, OFF), rows(ib, OFF - 1), rows(ib, OFF + 1)
+        first, last = edge_lanes(TALL)
+        at, mid = rows(ib, 0, TALL), rows(ib, OFF, TALL)
+        below, above = rows(ib, OFF - 1, TALL), rows(ib, OFF + 1, TALL)
         km_u = kmu[at, :]
         km_w = kmw[at, :]
         km_v = kmv[at, :]
@@ -478,22 +497,23 @@
             k = step
             if k < LEVELS:
                 sh = NJ - 1 - 2 * k
-                turned[k] = [(rot(q, sh), rot(q, sh - 1)) for _, _, q, _ in fields]
+                turned[k] = [rot(q, sh) for _, _, q, _ in fields]
             k = step - LAG
             if 0 <= k < LEVELS:
                 v = keep(km_v > k, v3[k, mid, :])
                 northward = v > 0
                 flux[k] = []
-                for (ref, next_ref, _, _), (north, south) in zip(fields, turned.pop(k)):
-                    xn = jnp.where(last8, north, next_ref[k, at, :])
+                for (ref, next_ref, _, _), halo in zip(fields, turned.pop(k)):
+                    xn = jnp.where(last, halo, next_ref[k, at, :])
                     fn = v * jnp.where(northward, ref[k, mid, :], xn)
-                    flux[k].append((fn, back(jnp.where(last8, south, fn))))
+                    flux[k].append((fn, back(fn), halo))
             k = step - 2 * LAG
             if k >= 0:
                 u = keep(km_u > k, u3[k, mid, :])
                 w = keep(km_w > k, u3[k, below, :])
                 eastward, from_west = u > 0, w > 0
-                for n, ((ref, _, _, out), (fn, fs)) in enumerate(zip(fields, flux.pop(k))):
+                for n, ((ref, _, _, out), (fn, fs, halo)) in enumerate(zip(fields, flux.pop(k))):
+                    fs = jnp.where(first, halo, fs)
                     x = ref[k, mid, :]
                     fe = u * jnp.where(eastward, x, ref[k, above, :])
                     fw = w * jnp.where(from_west, ref[k, below, :], x)
@@ -501,7 +521,7 @@
                     prev[n] = rhs + RATIO_D[k - 1] * prev[n] if k else rhs
                     out[k, at, :] = prev[n]
         return carry
-    lax.fori_loop(0, blocks, tracer_body, 0)
+    lax.fori_loop(0, NI // TALL, tracer_body, 0)
 
     recv(g2, g2a_n + gc_n, g2a_s + gc_s)
     low_ok = jnp.full((HALO, IEXT), has_sf) > 0.5

time: 30.9 us -> 29.9 us (0.968)
  Pallas kernels: 30.1 us -> 29.1 us
    pallas_call x1, Pallas kernels: 26.3 us -> 25.3 us  [ocean_step(): pl.pallas_call(functools.partial(exchange_kernel, col_count, row_count),...]
where the time goes in v2:
time: 29.9 us; the launch traced here: 29.7 us
  Pallas kernels  29.1 us (97%)
  between operations  0.64 us (2%)
    pallas_call x1, Pallas kernels, ocean_step(): pl.pallas_call(functools.partial(exchange_kernel, col_count, row_count),...  25.3 us
    pallas_call x1, Pallas kernels, ocean_step(): pl.pallas_call(back_kernel, out_shape=tuple((jax.ShapeDtypeStruct(flat, F...  3.79 us

profile of v2, /device:TPU:1, one launch (start us, length us, event | category | flops | bytes accessed | tf_op | source)
XLA Modules:
  0.0 29.7 jit_solution(17592132859251072659)
XLA Ops:
  0.6 25.3 %shard_map.144 = (f32[62,64,128]{2,1,0:T(8,128)S(1)}, f32[62,64,128]{2,1,0:T(8,128)S(1)}, f32[62,64,128]{2,1,0:T(8,128)S(1)}, f32[62,64,128]{2,1,0:T(8,128)S(1)}, f32[8,64,128]{2,1,0:T(8,128)S(1)}) custom-call(f32[62,64,128]{2,1,0:T(8,128)} %bitcast.16, f32[62,64,128]{2,1,0:T(8,128)} %bitcast.17, f32[62,64,128]{2,1,0:T(8,128)} %bitcast.18, ...), custom_call_target="tpu_custom_call" | custom-call | tf_op jit(solution)/shard_map/pallas_call | solution.py:685
  25.9 3.8 %shard_map.145 = (f32[64,128]{1,0:T(8,128)}, f32[64,128]{1,0:T(8,128)}, f32[64,128]{1,0:T(8,128)}, f32[62,64,128]{2,1,0:T(8,128)}, f32[62,64,128]{2,1,0:T(8,128)...) custom-call(f32[62,64,128]{2,1,0:T(8,128)S(1)} %get-tuple-element.19.du, f32[62,64,128]{2,1,0:T(8,128)S(1)} %get-tuple-element.20.dv, ...), custom_call_target="tpu_custom_call" | custom-call | tf_op jit(solution)/shard_map/pallas_call | solution.py:708

commit v3 on v2

--- a/solution.py
+++ b/solution.py
@@ -63,7 +63,7 @@
 WEIGHTS = sm_weights()
 TAIL_WEIGHTS = np.cumsum(WEIGHTS[::-1])[::-1]
 MEAN_STEP = float(np.sum(WEIGHTS * np.arange(1, SUBCYCLES + 1)))
-MESSAGES = 32
+MESSAGES = 33
 STAGGER = 500
 TALL = 16
 PARTS = ((0, 16), (16, 32), (32, 48), (48, LEVELS))
@@ -102,8 +102,9 @@
     return x / jnp.maximum(count, 1.0)
 
 
-ETA, TU, TV, WET_DEP = range(4)
-DEP, KMT = range(2)
+ETA, STEP, WET_DEP, TU, TV = range(5)
+WIDE = 3
+DEP, KMT, SOUTH_V = range(3)
 U, V, T, S, MEAN, PRES, T_FLUX, S_FLUX = range(8)
 UV, TS = range(2)
 
@@ -112,11 +113,11 @@
     col_count, row_count,
     u_hbm, v_hbm, t_hbm, s_hbm, eta_hbm, tu_hbm, tv_hbm, dep_hbm, kmt_hbm,
     du_o, dv_o, dt_o, ds_o, flat_o,
-    u3, v3, t3, s3, p3, un3, us3, vn3, vs3, tn3, sn3, st2, nd2, near_w, near_e, kmt_i, ext2, pk2n, pk2s, hs2, hn2,
+    u3, v3, t3, s3, p3, un3, us3, vn3, vs3, tn3, sn3, st2, nd2, near_w, near_e, near_u, kmt_i, ext2, pk2n, pk2s, hs2, hn2,
     pack, mn, ms, in_s, in_n, rr,
-    ff, extf, pkfn, pkfs, hsf, hnf,
+    ff, extf, pkfn, pkfs, hsf, hnf, fold, fold_in,
     kmu, kmw, kmv, hu2, hv2, smr,
-    b_e0, b_e1, b_d, b_p, b_wu, b_ww, b_wv, b_u, b_v, b_pu, b_pv, b_s, b_g,
+    b_e0, b_e1, b_d, b_p, b_wu, b_ww, b_wv, b_pu, b_pv, b_s, b_g,
     ld3, ld2, snd, rcv,
 ):
     c = lax.axis_index("col")
@@ -228,8 +229,8 @@
 
     def side_ew(own, ext):
         return [
-            remote(own.at[:, FAR_EAST, :], ext.at[:, LOW, :], east, r),
-            remote(own.at[:, FAR_WEST, :], ext.at[:, HIGH, :], west, r),
+            remote(own.at[:ext.shape[0], FAR_EAST, :], ext.at[:, LOW, :], east, r),
+            remote(own.at[:ext.shape[0], FAR_WEST, :], ext.at[:, HIGH, :], west, r),
         ]
 
     lane64 = lax.broadcasted_iota(jnp.int32, (NI, NJ), 1)
@@ -274,6 +275,7 @@
             spare = lane64 == SPARE + f
             top = jnp.where(spare, rot(x, SPARE + f + 1), top)
             bottom = jnp.where(spare, rot(x, SPARE + f), bottom)
+        top = jnp.where(lane64 == SPARE + SOUTH_V, rot(st2[TV], SPARE + SOUTH_V + 1), top)
         return top, bottom
 
     landed(0)
@@ -290,6 +292,7 @@
     g0 = [
         remote(nd2.at[:, EAST, :], near_w.at[:, WEST, :], east, r),
         remote(nd2.at[:, WEST, :], near_e.at[:, WEST, :], west, r),
+        remote(st2.at[TU:TU + 1, EAST, :], near_u.at[:, WEST, :], east, r),
     ]
     start(g0 + g1)
 
@@ -307,15 +310,6 @@
     g7n = [remote(mn.at[UV, :OFF, :], in_s.at[UV, AFTER, :], west, up)]
     g7s = [remote(ms.at[UV, NI - OFF:NI, :], in_n.at[UV, BEFORE, :], east, down)]
     start((), g5n + g7n, g5s + g7s)
-    wide2 = pk2n.at[0], pk2s.at[0], hs2.at[0], hn2.at[0]
-    pack_flat(range(4), st2, *wide2[:2])
-    g2 = side_ew(st2, ext2)
-    g2a_n, g2a_s = near_ns(*wide2)
-    gc_n, gc_s = corners(*wide2)
-    start(g2, g2a_n + gc_n, g2a_s + gc_s)
-    for f in range(4):
-        ext2[f, CORE, :] = st2[f]
-
     def local_body(ib, carry):
         mid, at = rows(ib, OFF, TALL), rows(ib, 0, TALL)
         km = nd2[KMT, at, :]
@@ -335,7 +329,9 @@
     blocks = NI // 8
     lax.fori_loop(0, NI // TALL, local_body, 0)
 
-    recv((), g3n, g3s)
+    recv(g0, g3n, g3s)
+    for f in (DEP, KMT):
+        nd2[f, NI:NI + 1, :] = near_e[f, WEST, :]
     has_nf = keep(has_n, 1.0).astype(F32)
     has_sf = keep(has_s, 1.0).astype(F32)
     big_n = jnp.full((NI, 1), has_nf) > 0.5
@@ -351,12 +347,26 @@
     kmv[...] = kmv_v
     hv2[...] = keep(kmv_v > 0, 0.5 * (depth + dep_north))
 
-    def u_faces():
-        kmu_v = jnp.minimum(nd2[KMT, :NI, :], nd2[KMT, 1:NI + 1, :])
-        kmu[...] = kmu_v
-        hu2[...] = keep(kmu_v > 0, 0.5 * (nd2[DEP, :NI, :] + nd2[DEP, 1:NI + 1, :]))
-
-    u_faces()
+    kmu_v = jnp.minimum(kmt, nd2[KMT, 1:NI + 1, :])
+    kmu[...] = kmu_v
+    hu2[...] = keep(kmu_v > 0, 0.5 * (depth + nd2[DEP, 1:NI + 1, :]))
+    first_col = lax.broadcasted_iota(jnp.int32, (NI, NJ), 0) == 0
+    kmw_v = jnp.minimum(kmt, jnp.where(first_col, near_w[KMT, WEST, :], pltpu.roll(kmt, 1, 0)))
+    kmw[...] = kmw_v
+
+    u0, v0 = keep(kmu_v > 0, st2[TU]), keep(kmv_v > 0, st2[TV])
+    u0_west = jnp.where(first_col, keep(kmw_v > 0, near_u[0, WEST, :]), pltpu.roll(u0, 1, 0))
+    v_s = in_s[TS, OWN, SPARE + SOUTH_V:SPARE + SOUTH_V + 1]
+    v0_south = jnp.where(lane64 == 0, keep(jnp.minimum(kmt_s, kmt) > 0, v_s), back(v0))
+    st2[STEP] = -WAVE_COURANT * ((u0 - u0_west) + (v0 - v0_south))
+    wide2 = pk2n.at[0], pk2s.at[0], hs2.at[0], hn2.at[0]
+    pack_flat(range(WIDE), st2, *wide2[:2])
+    g2 = side_ew(st2, ext2)
+    g2a_n, g2a_s = near_ns(*wide2)
+    gc_n, gc_s = corners(*wide2)
+    start(g2, g2a_n + gc_n, g2a_s + gc_s)
+    for f in range(WIDE):
+        ext2[f, CORE, :] = st2[f]
 
     def unpack_pair(a, where):
         north = keep(has_nf > 0.5, in_n[a, where, :])
@@ -448,13 +458,7 @@
         smr[1, at, :] = inv_v * sr_v
 
     def beside():
-        recv(g0 + g1, g7n, g7s)
-        for f in (DEP, KMT):
-            nd2[f, NI:NI + 1, :] = near_e[f, WEST, :]
-        u_faces()
-        kmt = nd2[KMT, :NI, :]
-        first_col = lax.broadcasted_iota(jnp.int32, (NI, NJ), 0) == 0
-        kmw[...] = jnp.minimum(kmt, jnp.where(first_col, near_w[KMT, WEST, :], pltpu.roll(kmt, 1, 0)))
+        recv(g1, g7n, g7s)
         unpack_pair(UV, BEFORE)
         unpack_pair(UV, AFTER)
         mean_rows()
@@ -478,7 +482,14 @@
     pack_flat((0, 1), ff, *force[:2])
     g4 = side_ew(ff, extf)
     g4_n, g4_s = near_ns(*force)
-    g6_n, g6_s = corners(*force)
+    half = HALO // 2
+    g6_n, g6_s = [], []
+    for n, (packed, row, out) in enumerate(((pkfn, up, g6_n), (pkfs, down, g6_s))):
+        for m, (near, far, cc) in enumerate((
+                (slice(NI - half, NI), slice(NI - HALO, NI - half), east),
+                (slice(0, half), slice(half, HALO), west))):
+            fold[n, m] = jnp.where(group64[:half] < 2, packed[0, near, :], rot(packed[0, far, :], 2 * HALO))
+            out.append(remote(fold.at[n, m], fold_in.at[n, m], cc, row))
     start(g4, g6_n + g4_n, g6_s + g4_s)
     for f in range(2):
         extf[f, CORE, :] = ff[f]
@@ -537,7 +548,7 @@
     north_of = pl.ds(9, JEXT)
     south_of = pl.ds(7, JEXT)
     zpad = jnp.zeros((8, IEXT), F32)
-    for ref in (b_e0, b_e1, b_wv, b_v, b_pv, b_s, b_g):
+    for ref in (b_e0, b_e1, b_wv, b_pv, b_s, b_g):
         ref[0:8, :] = zpad
         ref[8 + JEXT:16 + JEXT, :] = zpad
     dp_w = window(ext2[WET_DEP], hs_t, hn_t, WET_DEP)
@@ -551,13 +562,28 @@
     b_ww[...] = back(wu)
     b_wv[win, :] = wv
     b_e0[win, :] = keep(dp_w > 0, window(ext2[ETA], hs_t, hn_t, ETA))
-    u0 = keep(wet_u, window(ext2[TU], hs_t, hn_t, TU))
-    v0 = keep(wet_v, window(ext2[TV], hs_t, hn_t, TV))
-    b_u[...] = u0
-    b_v[win, :] = v0
-    b_d[...] = -WAVE_COURANT * ((u0 - back(u0)) + (v0 - b_v[south_of, :]))
+    b_d[...] = window(ext2[STEP], hs_t, hn_t, STEP)
+
+    def tracer_back(ib, carry):
+        at = rows(ib, 0, TALL)
+        kt = nd2[KMT, at, :]
+        xt = xs = jnp.zeros((TALL, NJ), F32)
+        for k in range(LEVELS - 1, -1, -1):
+            fac = jnp.where(kt > k + 1, INNER_D[k], keep(kt > k, LAST_D[k]))
+            xt = fac * dt_o[k, at, :] + RATIO_D[k] * xt
+            xs = fac * ds_o[k, at, :] + RATIO_D[k] * xs
+            dt_o[k, at, :] = xt
+            ds_o[k, at, :] = xs
+        return carry
+    lax.fori_loop(0, NI // TALL, tracer_back, 0)
 
     recv(g4, g4_n + g6_n, g4_s + g6_s)
+    for n, ref in enumerate((hsf, hnf)):
+        for m, (near, far) in enumerate((
+                (slice(half, HALO), slice(0, half)),
+                (slice(IEXT - HALO, IEXT - half), slice(IEXT - half, IEXT)))):
+            ref[0, near, :] = fold_in[n, m]
+            ref[0, far, :] = rot(fold_in[n, m], 2 * HALO)
     hsf_t = hsf[0].T
     hnf_t = hnf[0].T
     push = ADV_COURANT / SUBCYCLES
@@ -608,17 +634,17 @@
     flat_o[0] = last[mid, :].T[CORE]
     wu = b_wu[core, :] * 2.0
     wv = b_wv[mid, :] * 2.0
-    pu, pv, u0, v0 = b_pu[core, :], b_pv[mid, :], b_u[core, :], b_v[mid, :]
+    pu, pv = b_pu[core, :], b_pv[mid, :]
+    u0, v0 = keep(kmu[...] > 0, st2[TU]), keep(kmv[...] > 0, st2[TV])
     s, g = b_s[mid, :], b_g[mid, :]
-    flat_o[1] = (u0 + SUBCYCLES * pu - wu * (ahead(s) - s)).T[CORE]
-    flat_o[2] = (v0 + SUBCYCLES * pv - wv * (b_s[above, :] - s)).T[CORE]
-    mean_u = u0 + MEAN_STEP * pu - wu * (ahead(g) - g)
-    mean_v = v0 + MEAN_STEP * pv - wv * (b_g[above, :] - g)
+    flat_o[1] = u0 + (SUBCYCLES * pu - wu * (ahead(s) - s)).T[CORE]
+    flat_o[2] = v0 + (SUBCYCLES * pv - wv * (b_s[above, :] - s)).T[CORE]
+    mean_u = u0 + (MEAN_STEP * pu - wu * (ahead(g) - g)).T[CORE]
+    mean_v = v0 + (MEAN_STEP * pv - wv * (b_g[above, :] - g)).T[CORE]
     for f, (mean, depth_ref, km_ref) in enumerate(((mean_u, hu2, kmu), (mean_v, hv2, kmv))):
         d = depth_ref[...]
-        flat_o[3 + f] = mean.T[CORE] / jnp.where(d > 0, d, 1.0) - smr[f]
+        flat_o[3 + f] = mean / jnp.where(d > 0, d, 1.0) - smr[f]
         flat_o[5 + f] = km_ref[...]
-    flat_o[7] = nd2[KMT, :NI, :]
 
     sent(g0 + g1)
     sent(g2, g3n + g5n + g7n, g3s + g5s + g7s)
@@ -626,34 +652,30 @@
     sent(g4, g4_n + g6_n, g4_s + g6_s)
 
 
-CHUNKS = ((54, 62), (42, 54), (28, 42), (14, 28), (0, 14))
-
-
-def back_kernel(du, dv, dt, ds, flat, eta_h, tu_h, tv_h, u_h, v_h, t_h, s_h, xu, xv, xt, xs, sem2, sem3):
-    copies = [pltpu.make_async_copy(flat.at[f], out, sem2.at[f]) for f, out in enumerate((eta_h, tu_h, tv_h))]
+CHUNKS = ((42, LEVELS), (21, 42), (0, 21))
+
+
+def back_kernel(du, dv, t, s, flat, eta_h, tu_h, tv_h, u_h, v_h, t_h, s_h, xu, xv, sem2, sem3):
+    whole = ((t, t_h), (s, s_h), (flat.at[0], eta_h), (flat.at[1], tu_h), (flat.at[2], tv_h))
+    copies = [pltpu.make_async_copy(src, out, sem2.at[f]) for f, (src, out) in enumerate(whole)]
     for cp in copies:
         cp.start()
-    results = ((xu, u_h), (xv, v_h), (xt, t_h), (xs, s_h))
+    results = ((xu, u_h), (xv, v_h))
     for n, (lo, hi) in enumerate(CHUNKS):
         def body(ib, carry):
             rows = pl.ds(pl.multiple_of(ib * 8, 8), 8)
-            cu, cv, ku, kv, kt = (flat[f, rows, :] for f in range(3, 8))
-            x = [jnp.zeros((8, NJ), F32) if hi == LEVELS else ref[LEVELS, rows, :] for ref, _ in results]
+            cu, cv, ku, kv = (flat[f, rows, :] for f in range(3, 7))
+            x, y = (jnp.zeros((8, NJ), F32) if hi == LEVELS else ref[LEVELS, rows, :] for ref, _ in results)
             for k in range(hi - 1, lo - 1, -1):
                 wu, wv = ku > k, kv > k
                 fu = jnp.where(ku > k + 1, INNER_V[k], keep(wu, LAST_V[k]))
                 fv = jnp.where(kv > k + 1, INNER_V[k], keep(wv, LAST_V[k]))
-                ft = jnp.where(kt > k + 1, INNER_D[k], keep(kt > k, LAST_D[k]))
-                x[0] = fu * du[k, rows, :] + RATIO_V[k] * x[0]
-                x[1] = fv * dv[k, rows, :] + RATIO_V[k] * x[1]
-                x[2] = ft * dt[k, rows, :] + RATIO_D[k] * x[2]
-                x[3] = ft * ds[k, rows, :] + RATIO_D[k] * x[3]
-                xu[k, rows, :] = keep(wu, x[0] + cu)
-                xv[k, rows, :] = keep(wv, x[1] + cv)
-                xt[k, rows, :] = x[2]
-                xs[k, rows, :] = x[3]
-            for (ref, _), val in zip(results, x):
-                ref[LEVELS, rows, :] = val
+                x = fu * du[k, rows, :] + RATIO_V[k] * x
+                y = fv * dv[k, rows, :] + RATIO_V[k] * y
+                xu[k, rows, :] = keep(wu, x + cu)
+                xv[k, rows, :] = keep(wv, y + cv)
+            xu[LEVELS, rows, :] = x
+            xv[LEVELS, rows, :] = y
             return carry
         lax.fori_loop(0, NI // 8, body, 0)
         for f, (src, out) in enumerate(results):
@@ -678,27 +700,28 @@
         padded = VMEM((LEVELS, IPAD, NJ), F32)
         pair = VMEM((2,) + flat, F32)
         block = VMEM(cube, F32)
+        folded = VMEM((2, 2, HALO // 2, NJ), F32)
         single = VMEM((1,) + flat, F32)
         near = VMEM((2, OFF, NJ), F32)
         wide = VMEM((JEXT + 16, IEXT), F32)
         plain = VMEM((JEXT, IEXT), F32)
         inner = pl.pallas_call(
             functools.partial(exchange_kernel, col_count, row_count),
-            out_shape=tuple(VMEM(cube, F32) for _ in range(4)) + (VMEM((8,) + flat, F32),),
+            out_shape=tuple(VMEM(cube, F32) for _ in range(4)) + (VMEM((7,) + flat, F32),),
             in_specs=[hbm] * 9,
             out_specs=(vmem,) * 5,
             scratch_shapes=[
                 padded, padded, padded, padded, padded, padded, block, block, padded, block, block,
-                VMEM((4,) + flat, F32), VMEM((2, NI + OFF, NJ), F32), near, near, VMEM(flat, jnp.int32),
-                VMEM((4, IEXT, NJ), F32), single, single, VMEM((1, IEXT, NJ), F32), VMEM((1, IEXT, NJ), F32),
+                VMEM((5,) + flat, F32), VMEM((2, NI + OFF, NJ), F32), near, near, VMEM((1, OFF, NJ), F32),
+                VMEM(flat, jnp.int32), VMEM((WIDE, IEXT, NJ), F32), single, single, VMEM((1, IEXT, NJ), F32), VMEM((1, IEXT, NJ), F32),
                 VMEM((4,) + flat, F32), pair, pair,
                 VMEM((2, IPAD, NJ), F32), VMEM((2, IPAD, NJ), F32), VMEM((8, IPAD, NJ), F32),
                 pair, VMEM((2, IEXT, NJ), F32),
                 single, single,
-                VMEM((1, IEXT, NJ), F32), VMEM((1, IEXT, NJ), F32),
+                VMEM((1, IEXT, NJ), F32), VMEM((1, IEXT, NJ), F32), folded, folded,
                 VMEM(flat, F32), VMEM(flat, F32), VMEM(flat, F32),
                 VMEM(flat, F32), VMEM(flat, F32), pair,
-                wide, wide, plain, plain, plain, plain, wide, plain, wide, plain, wide, wide, wide,
+                wide, wide, plain, plain, plain, plain, wide, plain, wide, wide, wide,
                 dma((4, len(PARTS))), dma((5,)), dma((MESSAGES,)), dma((MESSAGES,)),
             ],
             compiler_params=pltpu.CompilerParams(
@@ -711,7 +734,7 @@
             + tuple(jax.ShapeDtypeStruct(cube, F32) for _ in range(4)),
             in_specs=[vmem] * 5,
             out_specs=(hbm,) * 7,
-            scratch_shapes=[spare, spare, spare, spare, dma((3,)), dma((len(CHUNKS), 4))],
+            scratch_shapes=[spare, spare, dma((5,)), dma((len(CHUNKS), 2))],
             compiler_params=pltpu.CompilerParams(vmem_limit_bytes=40 * 2 ** 20),
         )(*inner)
         return tuple(jnp.swapaxes(x, -1, -2) for x in outs)

time: 29.9 us -> 28.8 us (0.963)
  Pallas kernels: 29.1 us -> 28 us
    pallas_call x1, Pallas kernels: 25.3 us -> 24.6 us  [ocean_step(): pl.pallas_call(functools.partial(exchange_kernel, col_count, row_count),...]
    pallas_call x1, Pallas kernels: 3.79 us -> 3.35 us  [ocean_step(): pl.pallas_call(back_kernel, out_shape=tuple((jax.ShapeDtypeStruct(flat, F...]
where the time goes in v3:
time: 28.8 us; the launch traced here: 28.6 us
  Pallas kernels  28 us (97%)
  between operations  0.64 us (2%)
    pallas_call x1, Pallas kernels, ocean_step(): pl.pallas_call(functools.partial(exchange_kernel, col_count, row_count),...  24.6 us
    pallas_call x1, Pallas kernels, ocean_step(): pl.pallas_call(back_kernel, out_shape=tuple((jax.ShapeDtypeStruct(flat, F...  3.35 us

profile of v3, /device:TPU:1, one launch (start us, length us, event | category | flops | bytes accessed | tf_op | source)
XLA Modules:
  0.0 28.6 jit_solution(7591560912687981782)
XLA Ops:
  0.6 24.6 %shard_map.144 = (f32[62,64,128]{2,1,0:T(8,128)S(1)}, f32[62,64,128]{2,1,0:T(8,128)S(1)}, f32[62,64,128]{2,1,0:T(8,128)S(1)}, f32[62,64,128]{2,1,0:T(8,128)S(1)}, f32[7,64,128]{2,1,0:T(8,128)S(1)}) custom-call(f32[62,64,128]{2,1,0:T(8,128)} %bitcast.16, f32[62,64,128]{2,1,0:T(8,128)} %bitcast.17, f32[62,64,128]{2,1,0:T(8,128)} %bitcast.18, ...), custom_call_target="tpu_custom_call" | custom-call | tf_op jit(solution)/shard_map/pallas_call | solution.py:708
  25.3 3.3 %shard_map.145 = (f32[64,128]{1,0:T(8,128)}, f32[64,128]{1,0:T(8,128)}, f32[64,128]{1,0:T(8,128)}, f32[62,64,128]{2,1,0:T(8,128)}, f32[62,64,128]{2,1,0:T(8,128)...) custom-call(f32[62,64,128]{2,1,0:T(8,128)S(1)} %get-tuple-element.19.du, f32[62,64,128]{2,1,0:T(8,128)S(1)} %get-tuple-element.20.dv, ...), custom_call_target="tpu_custom_call" | custom-call | tf_op jit(solution)/shard_map/pallas_call | solution.py:731

commit v4 on v3

--- a/solution.py
+++ b/solution.py
@@ -69,7 +69,7 @@
 PARTS = ((0, 16), (16, 32), (32, 48), (48, LEVELS))
 SPARE = 2 * LEVELS
 LAG_M = 2
-LAG = 4
+LAG = 6
 CHUNK = 24
 
 
@@ -479,8 +479,9 @@
     lax.fori_loop(0, blocks, loop_body, 0)
 
     force = pkfn.at[0], pkfs.at[0], hsf.at[0], hnf.at[0]
+    g4 = side_ew(ff, extf)
+    start(g4)
     pack_flat((0, 1), ff, *force[:2])
-    g4 = side_ew(ff, extf)
     g4_n, g4_s = near_ns(*force)
     half = HALO // 2
     g6_n, g6_s = [], []
@@ -490,7 +491,7 @@
                 (slice(0, half), slice(half, HALO), west))):
             fold[n, m] = jnp.where(group64[:half] < 2, packed[0, near, :], rot(packed[0, far, :], 2 * HALO))
             out.append(remote(fold.at[n, m], fold_in.at[n, m], cc, row))
-    start(g4, g6_n + g4_n, g6_s + g4_s)
+    start((), g6_n + g4_n, g6_s + g4_s)
     for f in range(2):
         extf[f, CORE, :] = ff[f]
 

time: 28.8 us -> 28.6 us (level)
  no operation moved by 1% of the time
where the time goes in v4:
time: 28.6 us; the launch traced here: 28.5 us
  Pallas kernels  27.8 us (97%)
  between operations  0.64 us (2%)
    pallas_call x1, Pallas kernels, ocean_step(): pl.pallas_call(functools.partial(exchange_kernel, col_count, row_count),...  24.5 us
    pallas_call x1, Pallas kernels, ocean_step(): pl.pallas_call(back_kernel, out_shape=tuple((jax.ShapeDtypeStruct(flat, F...  3.35 us

profile of v4, /device:TPU:1, one launch (start us, length us, event | category | flops | bytes accessed | tf_op | source)
XLA Modules:
  0.0 28.5 jit_solution(5971365357898976938)
XLA Ops:
  0.6 24.5 %shard_map.144 = (f32[62,64,128]{2,1,0:T(8,128)S(1)}, f32[62,64,128]{2,1,0:T(8,128)S(1)}, f32[62,64,128]{2,1,0:T(8,128)S(1)}, f32[62,64,128]{2,1,0:T(8,128)S(1)}, f32[7,64,128]{2,1,0:T(8,128)S(1)}) custom-call(f32[62,64,128]{2,1,0:T(8,128)} %bitcast.16, f32[62,64,128]{2,1,0:T(8,128)} %bitcast.17, f32[62,64,128]{2,1,0:T(8,128)} %bitcast.18, ...), custom_call_target="tpu_custom_call" | custom-call | tf_op jit(solution)/shard_map/pallas_call | solution.py:709
  25.1 3.3 %shard_map.145 = (f32[64,128]{1,0:T(8,128)}, f32[64,128]{1,0:T(8,128)}, f32[64,128]{1,0:T(8,128)}, f32[62,64,128]{2,1,0:T(8,128)}, f32[62,64,128]{2,1,0:T(8,128)...) custom-call(f32[62,64,128]{2,1,0:T(8,128)S(1)} %get-tuple-element.19.du, f32[62,64,128]{2,1,0:T(8,128)S(1)} %get-tuple-element.20.dv, ...), custom_call_target="tpu_custom_call" | custom-call | tf_op jit(solution)/shard_map/pallas_call | solution.py:732
